TPU v7x, 256 devices: a whole 4x4x8 slice. The times are simulated.
256 devices in a mesh: section: 32 (over z, y), dp: 4 (over x), mp: 2 (over core).
Axes of the slice: x: 4, y: 4, z: 8, core: 2. Of those that a mesh axis runs over, the one named last changes fastest.
Arguments:
- inputs: bfloat16 [4, 128, 8192], P(None, 'dp'), may hold values from -12.7 to 12.7
- value_weight: bfloat16 [32, 8192, 1024], P('section', None, 'mp'), may hold values from -0.13975425 to 0.13975425
- carry_gain: float32 [32, 8192], P('section'), may hold values from 0.6 to 1.4
- channel_bins: int32 [32, 8192], P('section'), may hold values from 0 to 15
- grid_picks: int32 [32, 20], P('section'), may hold values from 0 to 19, each once within a row
Outputs:
- quant_out: bfloat16 [32, 4, 128, 1024], P('section', None, 'dp', 'mp')
- grid_loss: float32 [32, 4], P('section')
Inputs may be any that keep to these rules, and one draw needn't show every extreme that they name: `grid_picks`: each row lists every grid point once.
All inputs are finite; a program needn't handle non-finite values.
Results may differ from a plain program's by a relative error of at most 0.029.
Values may be sent and summed in bfloat16 or wider, within the bound.
A program may use at most 192 MiB of HBM per device.

v0:
```python
import math

import jax
import jax.numpy as jnp
from jax import lax
from jax.sharding import PartitionSpec as P

D = 8192
KV = 1024
HEAD = 128
GROUP = 128
GRID = 20
PICKS = 4


EPS = 1e-06
LOSS_UNIT = 1000.0
TWO_PI = 2.0 * math.pi


def sent_to_all(value, axis):
    peers = lax.axis_size(axis)
    return lax.all_to_all(
        jnp.broadcast_to(value[None], (peers, *value.shape)), axis, 0, 0, tiled=True
    )


def over_copies(value, axis):
    everything = sent_to_all(value, axis)
    return jnp.sum(everything, axis=0)


def from_behind(block, axis, distance):
    devices = range(lax.axis_size(axis))
    route = [(i - distance, i) for i in devices if i - distance in devices]
    return lax.ppermute(block, axis, route)


def quantize(weight, channel_bin, grid_pick):
    exponent = grid_pick.astype(jnp.float32) / GRID
    scaling = jnp.exp2(exponent * channel_bin.astype(jnp.float32) / 4.0)
    scaled = weight.astype(jnp.float32) * scaling[:, None]
    blocks = scaled.reshape(scaled.shape[0] // GROUP, GROUP, scaled.shape[1])
    spacing = (jnp.max(jnp.abs(blocks), axis=1, keepdims=True) + EPS) / 7.0
    levels = blocks / spacing
    snapped = (levels - jnp.sin(TWO_PI * levels) / TWO_PI) * spacing
    return (snapped.reshape(scaled.shape) / scaling[:, None]).astype(jnp.bfloat16)


def repeat_heads(values):
    row_count, columns = values.shape
    head_view = values.reshape(row_count, columns // HEAD, 1, HEAD)
    spread = jnp.broadcast_to(head_view, (row_count, columns // HEAD, D // KV, HEAD))
    return spread.reshape(row_count, columns * (D // KV))


def local(inputs, value_weight, carry_gain, channel_bins, grid_picks):
    section_count = lax.axis_size("section")
    section_index = lax.axis_index("section")
    micro_count, row_count, model_width = inputs.shape
    weight = value_weight[0]
    gain_row = carry_gain[0]
    half_width = weight.shape[1]
    stacked = jnp.concatenate(
        [
            quantize(weight, channel_bins[0], grid_picks[0, pick_index])
            for pick_index in range(PICKS)
        ],
        axis=1,
    )
    residual_gain = 1.0 / math.sqrt(section_count)
    tick_count = section_count + micro_count - 1

    def grid_pass(stream):
        exact = jnp.dot(stream, weight, preferred_element_type=jnp.float32)
        candidate = jnp.dot(stream, stacked, preferred_element_type=jnp.float32).reshape(
            row_count, PICKS, half_width
        )
        errors = jnp.sum(jnp.square(candidate - exact[:, None, :]), axis=(0, 2))
        return (candidate[:, 0, :].astype(jnp.bfloat16), errors)

    def spare_pass(stream):
        return (jnp.zeros((row_count, half_width), jnp.bfloat16), jnp.zeros((PICKS,), jnp.float32))

    def advance(tick_index, state_tuple):
        received, outputs, totals = state_tuple
        slot_index = tick_index - section_index
        active = jnp.logical_and(slot_index >= 0, slot_index < micro_count)
        clamped = jnp.clip(slot_index, 0, micro_count - 1)
        entry_rows = lax.dynamic_index_in_dim(inputs, clamped, 0, keepdims=False)
        stream = jnp.where(section_index == 0, entry_rows, received)
        chosen, errors = lax.cond(active, grid_pass, spare_pass, stream)
        previous = lax.dynamic_index_in_dim(outputs, clamped, 0, keepdims=False)
        outputs = lax.dynamic_update_index_in_dim(
            outputs, jnp.where(active, chosen, previous), clamped, 0
        )
        totals = totals + over_copies(errors, ("dp", "mp"))
        part_width = model_width // lax.axis_size("mp")
        part_start = lax.axis_index("mp") * part_width
        own_features = lax.dynamic_slice_in_dim(stream, part_start, part_width, 1)
        own_gain = lax.dynamic_slice_in_dim(gain_row, part_start, part_width, 0)
        next_part = (
            own_features.astype(jnp.float32) * own_gain[None, :]
            + residual_gain * repeat_heads(chosen).astype(jnp.float32)
        ).astype(jnp.bfloat16)
        arrived = from_behind(next_part, "section", 1)
        received = lax.all_gather(arrived, "mp", axis=1, tiled=True)
        return (received, outputs, totals)

    initial = (
        jnp.zeros((row_count, model_width), jnp.bfloat16),
        jnp.zeros((micro_count, row_count, half_width), jnp.bfloat16),
        jnp.zeros((PICKS,), jnp.float32),
    )
    received, outputs, totals = lax.fori_loop(0, tick_count, advance, initial)
    entry_count = micro_count * row_count * lax.axis_size("dp") * half_width * lax.axis_size("mp")
    grid_loss = totals * LOSS_UNIT / entry_count
    return (outputs[None], grid_loss[None])


def solution(mesh):
    placed = (
        P(None, "dp", None),
        P("section", None, "mp"),
        P("section", None),
        P("section", None),
        P("section", None),
    )
    return jax.shard_map(
        local,
        mesh=mesh,
        in_specs=placed,
        out_specs=(P("section", None, "dp", "mp"), P("section", None)),
        check_vma=False,
    )
```

profile of v0, /device:TPU:249, one launch (start us, length us, event | category | flops | bytes accessed | tf_op | source)
XLA Modules:
  0.0 1431.0 jit_solution(17592622582749549896)
XLA Ops:
  5.6 12.4 fusion.11
  18.1 246.1 %fusion.3 = (bf16[8192,512]{1,0:T(8,128)(2,1)}, bf16[8192,512]{1,0:T(8,128)(2,1)}, bf16[8192,512]{1,0:T(8,128)(2,1)}, bf16[8192,512]{1,0:T(8,128)(2,1)}) fusion(f32[64,512]{1,0:T(8,128)S(1)} %get-tuple-element.292, f32[8192]{0:T(1024)S(1)} %bitcast.105, bf16[1,8192,512]{2,1,0:T(8,128)(2,1)} %param.10, f32[64,512]{1,0:T(8,128)S(1)} %get-tuple-element.289, ...), kind=kLoop, calls=%fused_computation.29 | loop fusion | flops 138412032 | bytes 42598400 | tf_op jit(solution)/shard_map/convert_element_type | solution.py:47
  264.2 22.7 %pad_maximum_fusion = bf16[8192,2048]{1,0:T(8,128)(2,1)} fusion(bf16[8192,512]{1,0:T(8,128)(2,1)} %get-tuple-element.278, bf16[8192,512]{1,0:T(8,128)(2,1)} %get-tuple-element.279, bf16[8192,512]{1,0:T(8,128)(2,1)} %get-tuple-element.280, bf16[8192,512]{1,0:T(8,128)(2,1)} %get-tuple-element.277), kind=kLoop, calls=%fused_computation.11 | loop fusion | flops 134217728 | bytes 67108864 | tf_op jit(solution)/shard_map/concatenate | solution.py:64
  287.0 1143.4 %while.19 = (s32[]{:T(128)}, bf16[32,8192]{1,0:T(8,128)(2,1)S(1)}, bf16[4,32,512]{2,1,0:T(8,128)(2,1)S(1)}, f32[4]{0:T(128)S(1)}, pred[]{:T(512)}, /*index=5*/s3...) while((s32[]{:T(128)}, bf16[32,8192]{1,0:T(8,128)(2,1)S(1)}, ...), condition=%wide.region_10.11_spmd.clone, body=%wide.region_4.10_spmd.clone.sunk | while | flops 1343275008 | bytes 50324384 | solution.py:115
  290.7 5.0 all-to-all-start
  309.9 4.5 all-to-all-done
  324.8 4.5 all-to-all-done
  399.3 4.5 all-to-all-done
  415.4 4.5 all-to-all-done
  496.1 4.5 all-to-all-done
  512.2 4.5 all-to-all-done
  609.0 4.5 all-to-all-done
  625.2 4.5 all-to-all-done
  705.8 4.5 all-to-all-done
  722.0 4.5 all-to-all-done
  774.9 509.6 %collective-permute-done = bf16[32,4096]{1,0:T(8,128)(2,1)S(1)} collective-permute-done((bf16[32,4096]{1,0:T(8,128)(2,1)S(1)}, bf16[32,4096]{1,0:T(8,128)(2,1)S(1)}, u32[]{:S(2)}, u32[]{:S(2)}) %collective-permute-start) | collective-permute-done | bytes 262176 | tf_op jit(solution)/shard_map/while/body/eval_jaxpr/ppermute | solution.py:36
  1288.3 19.0 %conditional.3 = (bf16[32,512]{1,0:T(8,128)(2,1)S(1)}, f32[4]{0:T(128)S(1)}, f32[32,512]{1,0:T(8,128)S(1)}) conditional(s32[]{:T(128)} %convert_element_type.178, () %tuple.72, (bf16[32,8192]{1,0:T(8,128)(2,1)S(1)}, bf16[8192,2048]{1,0:T(8,128)(2,1)}, bf16[8192,512]{1,0:T(8,128)(2,1)}) %tuple.73), branch_computations={%region_5.5_spmd, %region_6.8_spmd} | conditional | flops 1342455808 | bytes 44793900 | solution.py:92
  1288.3 4.9 fusion.20
  1293.4 13.6 multiply_reduce_fusion
  1309.6 4.9 all-to-all-start
  1324.6 19.0 %conditional.3 = (bf16[32,512]{1,0:T(8,128)(2,1)S(1)}, f32[4]{0:T(128)S(1)}, f32[32,512]{1,0:T(8,128)S(1)}) conditional(s32[]{:T(128)} %convert_element_type.178, () %tuple.72, (bf16[32,8192]{1,0:T(8,128)(2,1)S(1)}, bf16[8192,2048]{1,0:T(8,128)(2,1)}, bf16[8192,512]{1,0:T(8,128)(2,1)}) %tuple.73), branch_computations={%region_5.5_spmd, %region_6.8_spmd} | conditional | flops 1342455808 | bytes 44793900 | solution.py:92
  1324.6 4.9 fusion.20
  1329.7 13.6 multiply_reduce_fusion
  1345.9 4.9 all-to-all-start
  1360.8 19.0 %conditional.3 = (bf16[32,512]{1,0:T(8,128)(2,1)S(1)}, f32[4]{0:T(128)S(1)}, f32[32,512]{1,0:T(8,128)S(1)}) conditional(s32[]{:T(128)} %convert_element_type.178, () %tuple.72, (bf16[32,8192]{1,0:T(8,128)(2,1)S(1)}, bf16[8192,2048]{1,0:T(8,128)(2,1)}, bf16[8192,512]{1,0:T(8,128)(2,1)}) %tuple.73), branch_computations={%region_5.5_spmd, %region_6.8_spmd} | conditional | flops 1342455808 | bytes 44793900 | solution.py:92
  1360.8 4.9 fusion.20
  1365.9 13.6 multiply_reduce_fusion
  1382.1 4.9 all-to-all-start
  1397.1 19.0 %conditional.3 = (bf16[32,512]{1,0:T(8,128)(2,1)S(1)}, f32[4]{0:T(128)S(1)}, f32[32,512]{1,0:T(8,128)S(1)}) conditional(s32[]{:T(128)} %convert_element_type.178, () %tuple.72, (bf16[32,8192]{1,0:T(8,128)(2,1)S(1)}, bf16[8192,2048]{1,0:T(8,128)(2,1)}, bf16[8192,512]{1,0:T(8,128)(2,1)}) %tuple.73), branch_computations={%region_5.5_spmd, %region_6.8_spmd} | conditional | flops 1342455808 | bytes 44793900 | solution.py:92
  1397.1 4.9 fusion.20
  1402.2 13.6 multiply_reduce_fusion
  1418.4 4.9 all-to-all-start
  (708 shorter events, 490.8 us)
Async XLA Ops:
  288.8 11.4 collective-permute-start
  304.4 10.6 collective-permute-start
  334.2 10.5 collective-permute-start
  378.6 10.8 collective-permute-start
  393.8 11.8 collective-permute-start
  409.9 11.8 collective-permute-start
  426.0 11.8 collective-permute-start
  442.2 11.8 collective-permute-start
  458.3 11.8 collective-permute-start
  474.4 11.8 collective-permute-start
  490.6 11.8 collective-permute-start
  506.7 11.8 collective-permute-start
  522.8 11.8 collective-permute-start
  539.0 11.8 collective-permute-start
  555.1 11.8 collective-permute-start
  571.2 11.8 collective-permute-start
  587.4 11.8 collective-permute-start
  603.5 11.8 collective-permute-start
  619.6 11.8 collective-permute-start
  635.8 11.8 collective-permute-start
  651.9 11.8 collective-permute-start
  668.1 11.8 collective-permute-start
  684.2 11.8 collective-permute-start
  700.3 11.8 collective-permute-start
  716.5 11.8 collective-permute-start
  732.6 11.8 collective-permute-start
  748.7 11.8 collective-permute-start
  764.9 519.6 %collective-permute-start = (bf16[32,4096]{1,0:T(8,128)(2,1)S(1)}, bf16[32,4096]{1,0:T(8,128)(2,1)S(1)}, u32[]{:S(2)}, u32[]{:S(2)}) collective-permute-start(bf16[32,4096]{1,0:T(8,128)(2,1)S(1)} %fusion.27), channel_id=1, source_target_pairs={{0,8},{8,16},{16,24},{24,32},{32,40},{40,48},{48,56},{56,64},{64,7... | collective-permute-start | bytes 786440 | tf_op jit(solution)/shard_map/while/body/eval_jaxpr/ppermute | solution.py:36
  1307.7 13.0 collective-permute-start
  1344.0 13.0 collective-permute-start
  1380.2 13.0 collective-permute-start
  1416.5 11.4 collective-permute-start
  (40 other events, 346.0 us)
where the time goes:
time: 1440 us; the launch traced here: 1430 us
  waiting for transfers between devices  715 us (50%)
  other arithmetic  335 us (23%)
  starting transfers between devices  177 us (12%)
  blocking collectives  95.6 us (7%)
  matrix products  74 us (5%)
  local copies, waits for them, and re-layouts  27.1 us (2%)
    ppermute x35, waiting for transfers between devices, from_behind(): return lax.ppermute(block, axis, route)  556 us
    convert_element_type x1, other arithmetic, quantize(): (snapped.reshape(scaled.shape) / scaling[:, None]).astype(jnp.bfloat16)  246 us
    all_to_all x35, waiting for transfers between devices, sent_to_all(): lax.all_to_all(jnp.broadcast_to(value[None], (peers, *value.shape)), axis...  158 us
    all_to_all x35, starting transfers between devices, sent_to_all(): lax.all_to_all(jnp.broadcast_to(value[None], (peers, *value.shape)), axis...  132 us
    all_gather x35, blocking collectives, advance(): received = lax.all_gather(arrived, 'mp', axis=1, tiled=True)  95.6 us
    dot_general x4, matrix products, grid_pass(): jnp.dot(stream, stacked, preferred_element_type=jnp.float32)  54.4 us
    ppermute x35, starting transfers between devices, from_behind(): return lax.ppermute(block, axis, route)  45.2 us
    select_n x35, other arithmetic, advance(): stream = jnp.where(section_index == 0, entry_rows, received)  38.4 us
  transfers between devices with their start and end apart: 70, of which 68 were waited for; matrix products, arithmetic and copies ran while one was open for 2% of the time, Pallas kernels for 0%

commit v1 on v0

v1 whole, which is shorter than its diff:
```python
import math

import jax
import jax.numpy as jnp
from jax import lax
from jax.experimental import pallas as pl
from jax.experimental.pallas import tpu as pltpu
from jax.sharding import PartitionSpec as P

D = 8192
KV = 1024
HALF = 512
HEAD = 128
GROUP = 128
GRID = 20
PICKS = 4
MICRO = 4
ROWS = 16
LATE = 16

EPS = 1e-06
LOSS_UNIT = 1000.0
MESH = pl.DeviceIdType.MESH
SINE = (
    0.9999996039221354,
    -6.579691570017649,
    12.98643600013728,
    -12.188101534445755,
    6.558042246424786,
    -1.953032018015784,
)
F32 = jnp.float32
BF16 = jnp.bfloat16


def sine_part(levels):
    r = levels - jnp.round(levels)
    z = r * r
    acc = jnp.full_like(z, SINE[-1])
    for c in SINE[-2::-1]:
        acc = acc * z + c
    return acc * r


def spread_rows(row_block, count, out):
    columns = row_block.T
    for k in range(count):
        out[k] = jnp.broadcast_to(columns[:, k : k + 1], (GROUP, 128))


def spacing_of(w_ref, scale, start, cs):
    high = None
    for q in range(4):
        part = w_ref[pl.ds(pl.multiple_of(start + 32 * q, 32), 32), cs].astype(F32) * scale(q)
        part = jnp.max(jnp.abs(part), axis=0, keepdims=True)
        high = part if high is None else jnp.maximum(high, part)
    return high + EPS


def first_body(w_ref, v_ref, q_ref, m_ref, acc, wide):
    acc[...] = jnp.zeros_like(acc)

    def block(r, carry):
        spread_rows(v_ref[r], 5, wide)
        start = r * GROUP
        for c in range(4):
            cs = pl.ds(c * 128, 128)
            high = spacing_of(w_ref, lambda q: wide[0, pl.ds(32 * q, 32), :], start, cs)
            up = 7.0 / high
            down = high * (-1.0 / 7.0)
            for q in range(4):
                rows = pl.ds(32 * q, 32)
                at = pl.ds(pl.multiple_of(start + 32 * q, 32), 32)
                w = w_ref[at, cs].astype(F32)
                s = sine_part(w * wide[0, rows, :] * up)
                full = w + s * down * wide[1, rows, :]
                acc[0, rows, cs] += full
                acc[1, rows, cs] += full * wide[2, rows, :]
                acc[2, rows, cs] += full * wide[3, rows, :]
                q_ref[at, cs] = (full * wide[4, rows, :]).astype(BF16)
        return carry

    lax.fori_loop(0, 8, block, 0)
    m_ref[...] = (acc[...] * (1.0 / math.sqrt(32.0))).astype(BF16)


def first_pick(weight, vectors):
    return pl.pallas_call(
        first_body,
        grid=(8,),
        in_specs=[
            pl.BlockSpec((1024, HALF), lambda h: (h, 0)),
            pl.BlockSpec((8, 8, 128), lambda h: (h, 0, 0)),
        ],
        out_specs=[
            pl.BlockSpec((1024, HALF), lambda h: (h, 0)),
            pl.BlockSpec((3, HEAD, HALF), lambda h: (0, h, 0)),
        ],
        out_shape=[
            jax.ShapeDtypeStruct((D, HALF), BF16),
            jax.ShapeDtypeStruct((3, KV, HALF), BF16),
        ],
        scratch_shapes=[pltpu.VMEM((3, HEAD, HALF), F32), pltpu.VMEM((5, GROUP, 128), F32)],
        name="first_pick",
    )(weight, vectors)


def deltas_body(w_ref, v_ref, d_ref, wide):
    def block(r, carry):
        spread_rows(v_ref[r], 8, wide)
        start = r * GROUP
        for p in range(PICKS):
            for c in range(4):
                cs = pl.ds(c * 128, 128)
                high = spacing_of(w_ref, lambda q: wide[p, pl.ds(32 * q, 32), :], start, cs)
                up = 7.0 / high
                down = high * (-1.0 / 7.0)
                for q in range(4):
                    rows = pl.ds(32 * q, 32)
                    at = pl.ds(pl.multiple_of(start + 32 * q, 32), 32)
                    w = w_ref[at, cs].astype(F32)
                    s = sine_part(w * wide[p, rows, :] * up)
                    d_ref[p, at, cs] = (s * down * wide[PICKS + p, rows, :]).astype(BF16)
        return carry

    lax.fori_loop(0, 8, block, 0)


def deltas(weight, vectors):
    return pl.pallas_call(
        deltas_body,
        grid=(8,),
        in_specs=[
            pl.BlockSpec((1024, HALF), lambda h: (h, 0)),
            pl.BlockSpec((8, 8, 128), lambda h: (h, 0, 0)),
        ],
        out_specs=pl.BlockSpec((PICKS, 1024, HALF), lambda h: (0, h, 0)),
        out_shape=jax.ShapeDtypeStruct((PICKS, D, HALF), BF16),
        scratch_shapes=[pltpu.VMEM((8, GROUP, 128), F32)],
        name="deltas",
    )(weight, vectors)


def nothing(weight):
    return pl.pallas_call(
        lambda w_ref, d_ref: None,
        in_specs=[pl.BlockSpec(memory_space=pl.ANY)],
        out_specs=pl.BlockSpec(memory_space=pl.ANY),
        out_shape=jax.ShapeDtypeStruct((PICKS, D, HALF), BF16),
        name="nothing",
    )(weight)


def losses_body(s_ref, d_ref, o_ref, acc):
    @pl.when(pl.program_id(0) == 0)
    def _():
        acc[...] = jnp.zeros_like(acc)

    for p in range(PICKS):
        acc[p] += jnp.dot(s_ref[...], d_ref[p], preferred_element_type=F32)

    @pl.when(pl.program_id(0) == pl.num_programs(0) - 1)
    def _():
        rows = []
        for p in range(PICKS):
            total = jnp.sum(jnp.square(acc[p]), axis=0, keepdims=True)
            rows.append(total[:, :128] + total[:, 128:256] + total[:, 256:384] + total[:, 384:])
        o_ref[...] = jnp.concatenate(rows + rows, axis=0)


def losses(stream, delta):
    depth = 512
    return pl.pallas_call(
        losses_body,
        grid=(D // depth,),
        in_specs=[
            pl.BlockSpec((128, depth), lambda k: (0, k)),
            pl.BlockSpec((PICKS, depth, HALF), lambda k: (0, k, 0)),
        ],
        out_specs=pl.BlockSpec((8, 128), lambda k: (0, 0)),
        out_shape=jax.ShapeDtypeStruct((8, 128), F32),
        scratch_shapes=[pltpu.VMEM((PICKS, 128, HALF), F32)],
        name="losses",
    )(stream, delta)


def reduce_body(x_ref, o_ref, slots, send_sem, recv_sem):
    dp, mp = lax.axis_size("dp"), lax.axis_size("mp")
    peers = dp * mp
    rank = lax.axis_index("dp") * mp + lax.axis_index("mp")
    barrier = pltpu.get_barrier_semaphore()

    def place(k):
        other = lax.rem(rank + k, peers)
        return {"dp": lax.div(other, mp), "mp": lax.rem(other, mp)}

    for k in range(1, peers):
        pl.semaphore_signal(barrier, inc=1, device_id=place(k), device_id_type=MESH)
    pl.semaphore_wait(barrier, peers - 1)
    slots[0] = x_ref[...]
    copies = []
    for k in range(1, peers):
        copy = pltpu.make_async_remote_copy(
            src_ref=x_ref,
            dst_ref=slots.at[k],
            send_sem=send_sem.at[k],
            recv_sem=recv_sem.at[k],
            device_id=place(k),
            device_id_type=MESH,
        )
        copy.start()
        copies.append(copy)
    for copy in copies:
        copy.wait()
    total = jnp.zeros_like(o_ref)
    for source in range(peers):
        total = total + slots[lax.rem(rank - source + peers, peers)]
    o_ref[...] = total


def reduce_all(part):
    return pl.pallas_call(
        reduce_body,
        in_specs=[pl.BlockSpec(memory_space=pltpu.VMEM)],
        out_specs=pl.BlockSpec(memory_space=pltpu.VMEM),
        out_shape=jax.ShapeDtypeStruct((8, 128), F32),
        scratch_shapes=[
            pltpu.VMEM((8, 8, 128), F32),
            pltpu.SemaphoreType.DMA((8,)),
            pltpu.SemaphoreType.DMA((8,)),
        ],
        compiler_params=pltpu.CompilerParams(collective_id=1, has_side_effects=True),
        name="reduce_all",
    )(part)


def chain_body(
    x_ref, q_ref, m_ref, v_ref, after_ref,
    out_ref, s_ref,
    full, fold, bulk, ahead, seen, near, mine,
    q_sem, m_sem, x_sem, near_send, near_recv, bulk_send, bulk_recv, save_sem, pair_send, pair_recv,
):
    sections = lax.axis_size("section")
    sec = lax.axis_index("section")
    half = lax.axis_index("mp")
    root = 1.0 / math.sqrt(sections)
    partner = {"mp": 1 - half}

    for i in range(3):
        @pl.when(sec <= i)
        def _():
            near[i] = jnp.zeros_like(near.at[i])

    barrier = pltpu.get_barrier_semaphore()
    pl.semaphore_signal(barrier, inc=1, device_id=partner, device_id_type=MESH)
    count = jnp.int32(1)
    for step in (1, 2, 3, 4):
        @pl.when(sec + step < sections)
        def _():
            pl.semaphore_signal(barrier, inc=1, device_id={"section": sec + step}, device_id_type=MESH)

        @pl.when(sec >= step)
        def _():
            pl.semaphore_signal(barrier, inc=1, device_id={"section": sec - step}, device_id_type=MESH)

        count = count + jnp.where(sec + step < sections, 1, 0) + jnp.where(sec >= step, 1, 0)
    pl.semaphore_wait(barrier, count)

    q_local = pltpu.make_async_copy(q_ref, full.at[half], q_sem.at[0])
    q_other = pltpu.make_async_remote_copy(
        src_ref=q_ref, dst_ref=full.at[half], send_sem=q_sem.at[1], recv_sem=q_sem.at[2],
        device_id=partner, device_id_type=MESH,
    )
    m_local = pltpu.make_async_copy(m_ref, fold.at[half], m_sem.at[0])
    m_other = pltpu.make_async_remote_copy(
        src_ref=m_ref, dst_ref=fold.at[half], send_sem=m_sem.at[1], recv_sem=m_sem.at[2],
        device_id=partner, device_id_type=MESH,
    )
    q_other.start()
    m_other.start()
    q_local.start()
    m_local.start()

    own_rows = pl.ds(pl.multiple_of(half * ROWS, ROWS), ROWS)
    x_copy = pltpu.make_async_copy(x_ref.at[:, own_rows, :], bulk, x_sem)

    @pl.when(sec < 4)
    def _():
        x_copy.start()
        x_copy.wait()

    q_local.wait()
    q_other.wait()
    m_local.wait()
    m_other.wait()

    def near_copy(i, w, target):
        return pltpu.make_async_remote_copy(
            src_ref=mine.at[w], dst_ref=near.at[i, w], send_sem=near_send.at[i, w],
            recv_sem=near_recv.at[i, w], device_id=target, device_id_type=MESH,
        )

    def bulk_copy(w, target):
        return pltpu.make_async_remote_copy(
            src_ref=ahead.at[w], dst_ref=bulk.at[w], send_sem=bulk_send.at[w],
            recv_sem=bulk_recv.at[w], device_id=target, device_id_type=MESH,
        )

    def tail_copies(w):
        own_cols = pl.ds(pl.multiple_of(half * HALF, HALF), HALF)
        other_cols = pl.ds(pl.multiple_of((1 - half) * HALF, HALF), HALF)
        return (
            pltpu.make_async_copy(mine.at[w, :, own_cols], out_ref.at[w, own_rows, :], save_sem.at[0, w]),
            pltpu.make_async_copy(seen.at[w], s_ref.at[w, own_rows, :], save_sem.at[1, w]),
        ), (
            pltpu.make_async_remote_copy(
                src_ref=mine.at[w, :, other_cols], dst_ref=out_ref.at[w, own_rows, :],
                send_sem=pair_send.at[0, w], recv_sem=pair_recv.at[0, w],
                device_id=partner, device_id_type=MESH,
            ),
            pltpu.make_async_remote_copy(
                src_ref=seen.at[w], dst_ref=s_ref.at[w, own_rows, :],
                send_sem=pair_send.at[1, w], recv_sem=pair_recv.at[1, w],
                device_id=partner, device_id_type=MESH,
            ),
        )

    def wave(w, carry):
        @pl.when(sec >= 4)
        def _():
            bulk_copy(w, {"section": sec}).wait_recv()

        def deep(k, sums):
            cs = pl.ds(pl.multiple_of(k * 1024, 1024), 1024)
            piece = bulk[w, :, cs]
            return (
                sums[0] + jnp.dot(piece, full[0, cs, :], preferred_element_type=F32),
                sums[1] + jnp.dot(piece, full[1, cs, :], preferred_element_type=F32),
            )

        zero = jnp.zeros((ROWS, HALF), F32)
        sums = lax.fori_loop(0, 8, deep, (zero, zero))
        for i in (2, 1, 0):
            @pl.when(sec >= i + 1)
            def _():
                near_copy(i, w, {"section": sec}).wait_recv()

            piece = near[i, w]
            sums = (
                sums[0] + jnp.dot(piece, fold[0, i], preferred_element_type=F32),
                sums[1] + jnp.dot(piece, fold[1, i], preferred_element_type=F32),
            )
        mine[w, :, :HALF] = sums[0].astype(BF16)
        mine[w, :, HALF:] = sums[1].astype(BF16)
        for i in range(3):
            @pl.when(sec + i + 1 < sections)
            def _():
                near_copy(i, w, {"section": sec + i + 1}).start()

        def assemble(c, carry):
            heads = pl.ds(pl.multiple_of(c * HEAD, HEAD), HEAD)
            y1 = near[0, w, :, heads].astype(F32) * root
            y2 = near[1, w, :, heads].astype(F32)
            y3 = near[2, w, :, heads].astype(F32)
            y0 = mine[w, :, heads].astype(F32) * root
            for r in range(8):
                cs = pl.ds(pl.multiple_of(c * 1024 + r * HEAD, HEAD), HEAD)
                now = (
                    v_ref[0:1, cs] * bulk[w, :, cs].astype(F32)
                    + v_ref[1:2, cs] * y3 + v_ref[2:3, cs] * y2 + y1
                )
                seen[w, :, cs] = now.astype(BF16)
                ahead[w, :, cs] = (v_ref[3:4, cs] * now + y0).astype(BF16)
            return carry

        lax.fori_loop(0, 8, assemble, 0)

        @pl.when(sec + 4 < sections)
        def _():
            bulk_copy(w, {"section": sec + 4}).start()

        local, remote = tail_copies(w)
        for copy in remote + local:
            copy.start()
        return carry

    lax.fori_loop(0, MICRO, wave, 0)

    def finish(w, carry):
        for i in range(3):
            @pl.when(sec + i + 1 < sections)
            def _():
                near_copy(i, w, {"section": sec + i + 1}).wait_send()

        @pl.when(sec + 4 < sections)
        def _():
            bulk_copy(w, {"section": sec + 4}).wait_send()

        local, remote = tail_copies(w)
        for copy in local:
            copy.wait()
        for copy in remote:
            copy.wait()
        return carry

    lax.fori_loop(0, MICRO, finish, 0)


def chain(inputs, quant, folds, vectors, after):
    anywhere = pl.BlockSpec(memory_space=pl.ANY)
    dma = pltpu.SemaphoreType.DMA
    return pl.pallas_call(
        chain_body,
        in_specs=[anywhere, anywhere, anywhere, pl.BlockSpec(memory_space=pltpu.VMEM), anywhere],
        out_specs=[anywhere, anywhere],
        out_shape=[
            jax.ShapeDtypeStruct((MICRO, 32, HALF), BF16),
            jax.ShapeDtypeStruct((MICRO, 32, D), BF16),
        ],
        scratch_shapes=[
            pltpu.VMEM((2, D, HALF), BF16),
            pltpu.VMEM((2, 3, KV, HALF), BF16),
            pltpu.VMEM((MICRO, ROWS, D), BF16),
            pltpu.VMEM((MICRO, ROWS, D), BF16),
            pltpu.VMEM((MICRO, ROWS, D), BF16),
            pltpu.VMEM((3, MICRO, ROWS, KV), BF16),
            pltpu.VMEM((MICRO, ROWS, KV), BF16),
            dma((3,)),
            dma((3,)),
            dma,
            dma((3, MICRO)),
            dma((3, MICRO)),
            dma((MICRO,)),
            dma((MICRO,)),
            dma((2, MICRO)),
            dma((2, MICRO)),
            dma((2, MICRO)),
        ],
        compiler_params=pltpu.CompilerParams(
            collective_id=0, has_side_effects=True, vmem_limit_bytes=60 * 1024 * 1024
        ),
        name="chain",
    )(inputs, quant, folds, vectors, after)


def from_behind(block, distance):
    sections = lax.axis_size("section")
    route = [(i - distance, i) for i in range(distance, sections)]
    moved = lax.ppermute(block, "section", route)
    return jnp.where(lax.axis_index("section") >= distance, moved, 1.0)


def local(inputs, value_weight, carry_gain, channel_bins, grid_picks):
    sec = lax.axis_index("section")
    weight = value_weight[0]
    own = carry_gain[0]
    g1 = from_behind(own, 1)
    g2 = from_behind(own, 2)
    g3 = from_behind(own, 3)
    g12 = g1 * g2
    g123 = g12 * g3
    exponent = grid_picks[0, :PICKS].astype(F32) / GRID
    scaling = jnp.exp2(exponent[:, None] * channel_bins[0].astype(F32)[None, :] / 4.0)
    inverse = 1.0 / scaling
    one = jnp.ones_like(g1)
    by_block = jnp.stack([scaling[0], inverse[0], g1, g12, g123, one, one, one])
    by_block = by_block.reshape(8, D // GROUP, GROUP).transpose(1, 0, 2)
    quant, folds = first_pick(weight, by_block)
    picks = jnp.concatenate([scaling, inverse]).reshape(8, D // GROUP, GROUP).transpose(1, 0, 2)
    weight, picks, quant, folds = lax.optimization_barrier((weight, picks, quant, folds))
    early_delta = lax.cond(sec >= LATE, lambda: deltas(weight, picks), lambda: nothing(weight))
    root = 1.0 / math.sqrt(lax.axis_size("section"))
    rows = jnp.stack([g123, g12 * root, g1 * root, own])
    quant_out, stream = chain(inputs, quant, folds, rows, early_delta)
    flat = stream.reshape(MICRO * 32, D)
    part = lax.cond(
        sec >= LATE,
        lambda: losses(flat, early_delta),
        lambda: losses(flat, deltas(weight, picks)),
    )
    total = reduce_all(part)
    entry_count = inputs.shape[0] * inputs.shape[1] * lax.axis_size("dp") * KV
    grid_loss = jnp.sum(total[:PICKS], axis=1) * (LOSS_UNIT / entry_count)
    return (quant_out[None], grid_loss[None])


def solution(mesh):
    placed = (
        P(None, "dp", None),
        P("section", None, "mp"),
        P("section", None),
        P("section", None),
        P("section", None),
    )
    return jax.shard_map(
        local,
        mesh=mesh,
        in_specs=placed,
        out_specs=(P("section", None, "dp", "mp"), P("section", None)),
        check_vma=False,
    )
```

time: 1440 us -> 284 us (0.20)
  the two profiles are of different devices: /device:TPU:249 before, /device:TPU:121 now
where the time goes in v1:
time: 284 us
  Pallas kernels  264 us (93%)
  starting transfers between devices  10.6 us (4%)
  other arithmetic  3.92 us (1%)
    pallas_call x1, Pallas kernels, chain(): pl.pallas_call(chain_body, in_specs=[anywhere, anywhere, anywhere, pl.Blo...  132 us
    pallas_call x1, Pallas kernels, deltas(): pl.pallas_call(deltas_body, grid=(8,), in_specs=[pl.BlockSpec((1024, HALF...  69 us
    pallas_call x1, Pallas kernels, first_pick(): pl.pallas_call(first_body, grid=(8,), in_specs=[pl.BlockSpec((1024, HALF)...  35 us
    pallas_call x1, Pallas kernels, losses(): pl.pallas_call(losses_body, grid=(D // depth,), in_specs=[pl.BlockSpec((1...  18.3 us
    ppermute x3, starting transfers between devices, from_behind(): moved = lax.ppermute(block, 'section', route)  10.6 us
    pallas_call x1, Pallas kernels, reduce_all(): pl.pallas_call(reduce_body, in_specs=[pl.BlockSpec(memory_space=pltpu.VME...  9.38 us
  transfers between devices with their start and end apart: 3, of which 1 were waited for; matrix products, arithmetic and copies ran while one was open for 1% of the time, Pallas kernels for 0%

profile of v1, /device:TPU:121, one launch (start us, length us, event | category | flops | bytes accessed | tf_op | source)
XLA Modules:
  0.0 283.6 jit_solution(1719301596908497129)
XLA Ops:
  0.6 4.4 %collective-permute-start = (f32[8192]{0:T(1024)}, f32[8192]{0:T(1024)S(1)}, u32[]{:S(2)}, u32[]{:S(2)}) collective-permute-start(f32[8192]{0:T(1024)} %bitcast.39), channel_id=1, source_target_pairs={{0,8},{8,16},{16,24},{24,32},{32,40},{40,48},{48,56},{56,64},{64,7... | collective-permute-start | bytes 98312 | tf_op jit(solution)/shard_map/ppermute | solution.py:449
  5.1 4.2 %collective-permute-start.1 = (f32[8192]{0:T(1024)}, f32[8192]{0:T(1024)S(1)}, u32[]{:S(2)}, u32[]{:S(2)}) collective-permute-start(f32[8192]{0:T(1024)} %bitcast.40), channel_id=1, source_target_pairs={{0,16},{8,24},{16,32},{24,40},{32,48},{40,56},{48,64},{56,72},{64,... | collective-permute-start | bytes 98312 | tf_op jit(solution)/shard_map/ppermute | solution.py:449
  9.3 1.9 collective-permute-start.2
  11.2 0.8 convert_element_type.17
  12.0 0.7 multiply_bitcast_fusion.1
  12.7 0.1 multiply_exponential_fusion
  12.8 0.1 multiply_exponential_fusion.1
  13.0 0.1 maximum_bitcast_fusion
  13.1 0.0 collective-permute-done
  13.1 0.0 collective-permute-done.1
  13.1 2.2 collective-permute-done.2
  15.4 1.0 stack.37
  16.4 35.0 %first_pick.1 = (bf16[8192,512]{1,0:T(8,128)(2,1)}, bf16[3,1024,512]{2,1,0:T(8,128)(2,1)}) custom-call(bf16[8192,512]{1,0:T(8,128)(2,1)} %bitcast.23, f32[64,8,128]{2,1,0:T(8,128)} %bitcast.29), custom_call_target="tpu_custom_call" | custom-call | tf_op jit(solution)/shard_map/first_pick/pallas_call | solution.py:88
  51.5 0.0 copy-start.1
  51.5 0.8 copy-done.1
  52.2 0.8 pad_maximum_fusion.v_ref
  53.0 131.8 %chain.1 = (bf16[4,32,512]{2,1,0:T(8,128)(2,1)}, bf16[4,32,8192]{2,1,0:T(8,128)(2,1)S(1)}) custom-call(bf16[4,32,8192]{2,1,0:T(8,128)(2,1)} %x_ref.1, bf16[8192,512]{1,0:T(8,128)(2,1)} %get-tuple-element.40.q_ref, bf16[3,1024,512]{2,1,0:T(8,128)(2,1)} %get-tuple-element.41.m_ref, f32[4,8192]{1,0:T(4,128)} %pad_maximum_fusion.v_ref, ...), custom_call_target="tpu_custom_call" | custom-call | tf_op jit(solution)/shard_map/chain/pallas_call | solution.py:412
  184.9 0.0 copy-start
  184.9 87.4 %conditional.3 = (f32[8,128]{1,0:T(8,128)S(1)}) conditional(s32[]{:T(128)} %convert_element_type.18, (bf16[8192,512]{1,0:T(8,128)(2,1)}, f32[64,8,128]{2,1,0:T(8,128)S(1)}, bf16[128,8192]{1,0:T(8,128)(2,1)S(1)}) %tuple.38, (bf16[128,8192]{1,0:T(8,128)(2,1)S(1)}, bf16[4,8192,512]{2,1,0:T(8,128)(2,1)}) %tuple.39), branch_computations={%region_2.3_spmd, %region_3.4_spmd} | conditional | bytes 8 | solution.py:476
  184.9 69.0 %deltas.3.d_ref = bf16[4,8192,512]{2,1,0:T(8,128)(2,1)} custom-call(bf16[8192,512]{1,0:T(8,128)(2,1)} %get-tuple-element.24.w_ref, f32[64,8,128]{2,1,0:T(8,128)S(1)} %get-tuple-element.25.v_ref), custom_call_target="tpu_custom_call" | custom-call | tf_op jit(solution)/shard_map/cond/branch_0_fun/deltas/pallas_call | solution.py:130
  253.9 18.3 %losses.2 = f32[8,128]{1,0:T(8,128)S(1)} custom-call(bf16[128,8192]{1,0:T(8,128)(2,1)S(1)} %get-tuple-element.23.s_ref, bf16[4,8192,512]{2,1,0:T(8,128)(2,1)} %deltas.3.d_ref), custom_call_target="tpu_custom_call" | custom-call | tf_op jit(solution)/shard_map/cond/branch_0_fun/losses/pallas_call | solution.py:173
  272.3 9.4 %reduce_all.1 = f32[8,128]{1,0:T(8,128)} custom-call(f32[8,128]{1,0:T(8,128)S(1)} %get-tuple-element.58.x_ref), custom_call_target="tpu_custom_call" | custom-call | tf_op jit(solution)/shard_map/reduce_all/pallas_call | solution.py:222
  281.7 0.8 slice_reduce_fusion
  282.5 0.5 multiply_bitcast_fusion
  283.0 0.0 copy-done
  283.0 0.7 copy.12
  (8 shorter events, 0.1 us)
Async XLA Ops:
  0.6 12.4 %collective-permute-start = (f32[8192]{0:T(1024)}, f32[8192]{0:T(1024)S(1)}, u32[]{:S(2)}, u32[]{:S(2)}) collective-permute-start(f32[8192]{0:T(1024)} %bitcast.39), channel_id=1, source_target_pairs={{0,8},{8,16},{16,24},{24,32},{32,40},{40,48},{48,56},{56,64},{64,7... | collective-permute-start | bytes 98312 | tf_op jit(solution)/shard_map/ppermute | solution.py:449
  5.1 8.0 %collective-permute-start.1 = (f32[8192]{0:T(1024)}, f32[8192]{0:T(1024)S(1)}, u32[]{:S(2)}, u32[]{:S(2)}) collective-permute-start(f32[8192]{0:T(1024)} %bitcast.40), channel_id=1, source_target_pairs={{0,16},{8,24},{16,32},{24,40},{32,48},{40,56},{48,64},{56,72},{64,... | collective-permute-start | bytes 98312 | tf_op jit(solution)/shard_map/ppermute | solution.py:449
  9.3 6.1 %collective-permute-start.2 = (f32[8192]{0:T(1024)}, f32[8192]{0:T(1024)S(1)}, u32[]{:S(2)}, u32[]{:S(2)}) collective-permute-start(f32[8192]{0:T(1024)} %bitcast.41), channel_id=1, source_target_pairs={{0,24},{8,32},{16,40},{24,48},{32,56},{40,64},{48,72},{56,80},{64,... | collective-permute-start | bytes 98312 | tf_op jit(solution)/shard_map/ppermute | solution.py:449
  51.5 0.8 copy-start.1
  184.9 98.1 %copy-start = (bf16[4,32,512]{2,1,0:T(8,128)(2,1)S(1)}, bf16[4,32,512]{2,1,0:T(8,128)(2,1)}, u32[]{:S(2)}) copy-start(bf16[4,32,512]{2,1,0:T(8,128)(2,1)} %get-tuple-element.44) | copy-start | bytes 393220

commit v2 on v1

v2 whole, which is shorter than its diff:
```python
import functools
import math

import jax
import jax.numpy as jnp
from jax import lax
from jax.experimental import pallas as pl
from jax.experimental.pallas import tpu as pltpu
from jax.sharding import PartitionSpec as P

D = 8192
KV = 1024
HALF = 512
HEAD = 128
GROUP = 128
GRID = 20
PICKS = 4
MICRO = 4
ROWS = 16
BEFORE = (10, 15, 20, 25)

EPS = 1e-06
LOSS_UNIT = 1000.0
MESH = pl.DeviceIdType.MESH
SINE = (
    0.9999996039221354,
    -6.579691570017649,
    12.98643600013728,
    -12.188101534445755,
    6.558042246424786,
    -1.953032018015784,
)
F32 = jnp.float32
BF16 = jnp.bfloat16


def sine_part(levels):
    r = levels - jnp.round(levels)
    z = r * r
    acc = jnp.full_like(z, SINE[-1])
    for c in SINE[-2::-1]:
        acc = acc * z + c
    return acc * r


def high_of(w_ref, wide, r, start, cs):
    high = None
    for q in range(4):
        part = w_ref[pl.ds(pl.multiple_of(start + 32 * q, 32), 32), cs].astype(F32)
        part = jnp.abs(part * wide[r, pl.ds(32 * q, 32), :])
        part = jnp.max(part, axis=0, keepdims=True)
        high = part if high is None else jnp.maximum(high, part)
    return high + EPS


def scales_of(bins, pick, wide, back):
    exponent = jnp.full(bins.shape, pick, jnp.int32).astype(F32) / GRID
    scaling = jnp.exp2(exponent * bins.astype(F32) / 4.0)
    columns, inverse = scaling.T, (1.0 / scaling).T
    for r in range(8):
        wide[r] = jnp.broadcast_to(columns[:, r : r + 1], (GROUP, 128))
        back[r] = jnp.broadcast_to(inverse[:, r : r + 1], (GROUP, 128))


def rounding_part(w, scale, back, up, down):
    return sine_part(w * scale * up) * down * back


def first_body(picks_ref, bins_ref, g_ref, w_ref, x_ref, q_ref, m_ref, a_ref, wide, back, left, acc):
    head = pl.program_id(0)
    scales_of(bins_ref[...], picks_ref[0, 0], wide, back)
    eye = lax.broadcasted_iota(jnp.int32, (HEAD, HEAD), 0) == lax.broadcasted_iota(jnp.int32, (HEAD, HEAD), 1)
    for r in range(8):
        cs = pl.ds(r * HEAD, HEAD)
        row = jnp.ones((1, HEAD), F32)
        for i, gain in enumerate((row, g_ref[2, r : r + 1, :], g_ref[1, r : r + 1, :])):
            left[i * HEAD : (i + 1) * HEAD, cs] = jnp.where(eye, gain, 0.0).astype(BF16)
        for w in range(MICRO):
            left[384 + w * 32 : 416 + w * 32, cs] = (
                x_ref[w, :, cs].astype(F32) * g_ref[0, r : r + 1, :]
            ).astype(BF16)

    def block(r, carry):
        start = r * GROUP
        for c in range(4):
            cs = pl.ds(c * 128, 128)
            high = high_of(w_ref, wide, r, start, cs)
            up = 7.0 / high
            down = high * (-1.0 / 7.0)
            for q in range(4):
                rows = pl.ds(32 * q, 32)
                at = pl.ds(pl.multiple_of(start + 32 * q, 32), 32)
                w = w_ref[at, cs].astype(F32)
                q_ref[at, cs] = (w + rounding_part(w, wide[r, rows, :], back[r, rows, :], up, down)).astype(BF16)
        return carry

    lax.fori_loop(0, 8, block, 0)
    product = jnp.dot(left[...], q_ref[...], preferred_element_type=F32)
    for i in range(3):
        m_ref[i] = (product[i * HEAD : (i + 1) * HEAD] * (1.0 / math.sqrt(32.0))).astype(BF16)

    @pl.when(head == 0)
    def _():
        acc[...] = product[384:]

    @pl.when(head > 0)
    def _():
        acc[...] += product[384:]

    @pl.when(head == 7)
    def _():
        for w in range(MICRO):
            a_ref[w] = acc[w * 32 : w * 32 + 32]


def first_pick(picks, bins, gains, weight, inputs):
    return pl.pallas_call(
        first_body,
        grid=(8,),
        in_specs=[
            pl.BlockSpec(memory_space=pltpu.SMEM),
            pl.BlockSpec((8, 128), lambda h: (h, 0)),
            pl.BlockSpec((4, 8, 128), lambda h: (0, h, 0)),
            pl.BlockSpec((1024, HALF), lambda h: (h, 0)),
            pl.BlockSpec((MICRO, 32, 1024), lambda h: (0, 0, h)),
        ],
        out_specs=[
            pl.BlockSpec((1024, HALF), lambda h: (h, 0)),
            pl.BlockSpec((3, HEAD, HALF), lambda h: (0, h, 0)),
            pl.BlockSpec((MICRO, 32, HALF), lambda h: (0, 0, 0)),
        ],
        out_shape=[
            jax.ShapeDtypeStruct((D, HALF), BF16),
            jax.ShapeDtypeStruct((3, KV, HALF), BF16),
            jax.ShapeDtypeStruct((MICRO, 32, HALF), F32),
        ],
        scratch_shapes=[
            pltpu.VMEM((8, GROUP, 128), F32),
            pltpu.VMEM((8, GROUP, 128), F32),
            pltpu.VMEM((512, 1024), BF16),
            pltpu.VMEM((128, HALF), F32),
        ],
        name="first_pick",
    )(picks, bins, gains, weight, inputs)


def picks_before(sec):
    return sum(jnp.where(sec >= least, 1, 0) for least in BEFORE)


def deltas_body(later, picks_ref, bins_ref, w_ref, old_ref, after_ref, d_ref, held, made, wide, back, w_sem, d_sem):
    split = picks_before(lax.axis_index("section"))
    low, count = (split, (PICKS - split) * 8) if later else (0, split * 8)

    def fetch(h):
        at = pl.ds(pl.multiple_of(h * 1024, 1024), 1024)
        return pltpu.make_async_copy(w_ref.at[at, :], held.at[at, :], w_sem.at[h])

    def put(t):
        at = pl.ds(pl.multiple_of(lax.rem(t, 8) * 1024, 1024), 1024)
        slot = lax.rem(t, 2)
        return pltpu.make_async_copy(made.at[slot], d_ref.at[low + lax.div(t, 8), at, :], d_sem.at[slot])

    @pl.when(count > 0)
    def _():
        for h in range(8):
            fetch(h).start()

    def step(t, carry):
        h = lax.rem(t, 8)
        slot = lax.rem(t, 2)

        @pl.when(t < 8)
        def _():
            fetch(h).wait()

        @pl.when(t >= 2)
        def _():
            put(t - 2).wait()

        scales_of(bins_ref[pl.ds(pl.multiple_of(h * 8, 8), 8), :], picks_ref[0, low + lax.div(t, 8)], wide, back)

        def block(r, carry):
            start = h * 1024 + r * GROUP
            for c in range(4):
                cs = pl.ds(c * 128, 128)
                high = high_of(held, wide, r, start, cs)
                up = 7.0 / high
                down = high * (-1.0 / 7.0)
                for q in range(4):
                    rows = pl.ds(32 * q, 32)
                    w = held[pl.ds(pl.multiple_of(start + 32 * q, 32), 32), cs].astype(F32)
                    made[slot, pl.ds(pl.multiple_of(r * GROUP + 32 * q, 32), 32), cs] = rounding_part(
                        w, wide[r, rows, :], back[r, rows, :], up, down
                    ).astype(BF16)
            return carry

        lax.fori_loop(0, 8, block, 0)
        put(t).start()
        return carry

    lax.fori_loop(0, count, step, 0)

    @pl.when(count > 0)
    def _():
        put(count - 2).wait()
        put(count - 1).wait()


def deltas(later, picks, bins, weight, old, after):
    anywhere = pl.BlockSpec(memory_space=pl.ANY)
    return pl.pallas_call(
        functools.partial(deltas_body, later),
        in_specs=[
            pl.BlockSpec(memory_space=pltpu.SMEM),
            pl.BlockSpec(memory_space=pltpu.VMEM),
            anywhere,
            anywhere,
            anywhere,
        ],
        out_specs=anywhere,
        out_shape=jax.ShapeDtypeStruct((PICKS, D, HALF), BF16),
        input_output_aliases={3: 0} if later else {},
        scratch_shapes=[
            pltpu.VMEM((D, HALF), BF16),
            pltpu.VMEM((2, 1024, HALF), BF16),
            pltpu.VMEM((8, GROUP, 128), F32),
            pltpu.VMEM((8, GROUP, 128), F32),
            pltpu.SemaphoreType.DMA((8,)),
            pltpu.SemaphoreType.DMA((2,)),
        ],
        name="deltas_later" if later else "deltas_before",
    )(picks, bins, weight, old, after)


def losses_body(s_ref, d_ref, o_ref, acc):
    part = pl.program_id(1)
    product = jnp.dot(s_ref[part], d_ref[0], preferred_element_type=F32)

    @pl.when(part == 0)
    def _():
        acc[...] = product

    @pl.when(part > 0)
    def _():
        acc[...] += product

    @pl.when(part == pl.num_programs(1) - 1)
    def _():
        total = jnp.sum(jnp.square(acc[...]), axis=0, keepdims=True)
        total = total[:, :128] + total[:, 128:256] + total[:, 256:384] + total[:, 384:]
        o_ref[pl.ds(pl.program_id(0), 1), :] = total


def losses(stream, delta):
    depth = 2048
    parts = D // depth
    return pl.pallas_call(
        losses_body,
        grid=(PICKS, parts),
        in_specs=[
            pl.BlockSpec((parts, 128, depth), lambda p, k: (0, 0, 0)),
            pl.BlockSpec((1, depth, HALF), lambda p, k: (p, k, 0)),
        ],
        out_specs=pl.BlockSpec((8, 128), lambda p, k: (0, 0)),
        out_shape=jax.ShapeDtypeStruct((8, 128), F32),
        scratch_shapes=[pltpu.VMEM((128, HALF), F32)],
        name="losses",
    )(stream, delta)


def gains_body(own_ref, o_ref, got, send_sem, recv_sem):
    sections = lax.axis_size("section")
    sec = lax.axis_index("section")
    for i in range(3):
        @pl.when(sec <= i)
        def _():
            got[i] = jnp.ones_like(own_ref)

    barrier = pltpu.get_barrier_semaphore()
    count = jnp.int32(0)
    for step in (1, 2, 3):
        @pl.when(sec + step < sections)
        def _():
            pl.semaphore_signal(barrier, inc=1, device_id={"section": sec + step}, device_id_type=MESH)

        @pl.when(sec >= step)
        def _():
            pl.semaphore_signal(barrier, inc=1, device_id={"section": sec - step}, device_id_type=MESH)

        count = count + jnp.where(sec + step < sections, 1, 0) + jnp.where(sec >= step, 1, 0)
    pl.semaphore_wait(barrier, count)

    def copy(i):
        return pltpu.make_async_remote_copy(
            src_ref=own_ref, dst_ref=got.at[i], send_sem=send_sem.at[i], recv_sem=recv_sem.at[i],
            device_id={"section": jnp.minimum(sec + i + 1, sections - 1)}, device_id_type=MESH,
        )

    for i in range(3):
        @pl.when(sec + i + 1 < sections)
        def _():
            copy(i).start()

    for i in range(3):
        @pl.when(sec > i)
        def _():
            copy(i).wait_recv()

    g1 = got[0]
    g12 = g1 * got[1]
    o_ref[0] = g12 * got[2]
    o_ref[1] = g12
    o_ref[2] = g1
    o_ref[3] = own_ref[...]
    for i in range(3):
        @pl.when(sec + i + 1 < sections)
        def _():
            copy(i).wait_send()


def gains_of(own):
    return pl.pallas_call(
        gains_body,
        in_specs=[pl.BlockSpec(memory_space=pltpu.VMEM)],
        out_specs=pl.BlockSpec(memory_space=pltpu.VMEM),
        out_shape=jax.ShapeDtypeStruct((4, D // 128, 128), F32),
        scratch_shapes=[
            pltpu.VMEM((3, D // 128, 128), F32),
            pltpu.SemaphoreType.DMA((3,)),
            pltpu.SemaphoreType.DMA((3,)),
        ],
        compiler_params=pltpu.CompilerParams(collective_id=2, has_side_effects=True),
        name="gains",
    )(own)


def reduce_body(x_ref, o_ref, slots, send_sem, recv_sem):
    dp, mp = lax.axis_size("dp"), lax.axis_size("mp")
    peers = dp * mp
    rank = lax.axis_index("dp") * mp + lax.axis_index("mp")
    barrier = pltpu.get_barrier_semaphore()

    def place(k):
        other = lax.rem(rank + k, peers)
        return {"dp": lax.div(other, mp), "mp": lax.rem(other, mp)}

    for k in range(1, peers):
        pl.semaphore_signal(barrier, inc=1, device_id=place(k), device_id_type=MESH)
    pl.semaphore_wait(barrier, peers - 1)
    slots[0] = x_ref[...]
    copies = []
    for k in range(1, peers):
        copy = pltpu.make_async_remote_copy(
            src_ref=x_ref,
            dst_ref=slots.at[k],
            send_sem=send_sem.at[k],
            recv_sem=recv_sem.at[k],
            device_id=place(k),
            device_id_type=MESH,
        )
        copy.start()
        copies.append(copy)
    for copy in copies:
        copy.wait()
    total = jnp.zeros_like(o_ref)
    for source in range(peers):
        total = total + slots[lax.rem(rank - source + peers, peers)]
    o_ref[...] = total


def reduce_all(part):
    return pl.pallas_call(
        reduce_body,
        in_specs=[pl.BlockSpec(memory_space=pltpu.VMEM)],
        out_specs=pl.BlockSpec(memory_space=pltpu.VMEM),
        out_shape=jax.ShapeDtypeStruct((8, 128), F32),
        scratch_shapes=[
            pltpu.VMEM((8, 8, 128), F32),
            pltpu.SemaphoreType.DMA((8,)),
            pltpu.SemaphoreType.DMA((8,)),
        ],
        compiler_params=pltpu.CompilerParams(collective_id=1, has_side_effects=True),
        name="reduce_all",
    )(part)


def chain_body(
    x_ref, q_ref, m_ref, a_ref, v_ref, after_ref,
    out_ref, s_ref,
    full, fold, start, bulk, ahead, seen, near, mine,
    q_sem, m_sem, a_sem, x_sem, near_send, near_recv, bulk_send, bulk_recv, save_sem, pair_send, pair_recv,
):
    sections = lax.axis_size("section")
    sec = lax.axis_index("section")
    half = lax.axis_index("mp")
    root = 1.0 / math.sqrt(sections)
    partner = {"mp": 1 - half}

    for i in range(3):
        @pl.when(sec <= i)
        def _():
            near[i] = jnp.zeros_like(near.at[i])

    barrier = pltpu.get_barrier_semaphore()
    pl.semaphore_signal(barrier, inc=1, device_id=partner, device_id_type=MESH)
    count = jnp.int32(1)
    for step in (1, 2, 3, 4):
        @pl.when(sec + step < sections)
        def _():
            pl.semaphore_signal(barrier, inc=1, device_id={"section": sec + step}, device_id_type=MESH)

        @pl.when(sec >= step)
        def _():
            pl.semaphore_signal(barrier, inc=1, device_id={"section": sec - step}, device_id_type=MESH)

        count = count + jnp.where(sec + step < sections, 1, 0) + jnp.where(sec >= step, 1, 0)
    pl.semaphore_wait(barrier, count)

    q_local = pltpu.make_async_copy(q_ref, full.at[half], q_sem.at[0])
    q_other = pltpu.make_async_remote_copy(
        src_ref=q_ref, dst_ref=full.at[half], send_sem=q_sem.at[1], recv_sem=q_sem.at[2],
        device_id=partner, device_id_type=MESH,
    )
    m_local = pltpu.make_async_copy(m_ref, fold.at[half], m_sem.at[0])
    m_other = pltpu.make_async_remote_copy(
        src_ref=m_ref, dst_ref=fold.at[half], send_sem=m_sem.at[1], recv_sem=m_sem.at[2],
        device_id=partner, device_id_type=MESH,
    )
    own_rows = pl.ds(pl.multiple_of(half * ROWS, ROWS), ROWS)
    other_rows = pl.ds(pl.multiple_of((1 - half) * ROWS, ROWS), ROWS)
    a_local = pltpu.make_async_copy(a_ref.at[:, own_rows, :], start.at[half], a_sem.at[0])
    a_other = pltpu.make_async_remote_copy(
        src_ref=a_ref.at[:, other_rows, :], dst_ref=start.at[half], send_sem=a_sem.at[1], recv_sem=a_sem.at[2],
        device_id=partner, device_id_type=MESH,
    )
    x_copy = pltpu.make_async_copy(x_ref.at[:, own_rows, :], bulk, x_sem)
    a_other.start()
    m_other.start()
    a_local.start()
    m_local.start()

    @pl.when(sec < 4)
    def _():
        x_copy.start()
        x_copy.wait()

    @pl.when(sec >= 4)
    def _():
        q_other.start()
        q_local.start()

    a_local.wait()
    a_other.wait()

    @pl.when(sec >= 1)
    def _():
        m_local.wait()
        m_other.wait()

    @pl.when(sec >= 4)
    def _():
        q_local.wait()
        q_other.wait()

    def near_copy(i, w, target):
        return pltpu.make_async_remote_copy(
            src_ref=mine.at[w], dst_ref=near.at[i, w], send_sem=near_send.at[i, w],
            recv_sem=near_recv.at[i, w], device_id=target, device_id_type=MESH,
        )

    def bulk_copy(w, target):
        return pltpu.make_async_remote_copy(
            src_ref=ahead.at[w], dst_ref=bulk.at[w], send_sem=bulk_send.at[w],
            recv_sem=bulk_recv.at[w], device_id=target, device_id_type=MESH,
        )

    def tail_copies(w):
        own_cols = pl.ds(pl.multiple_of(half * HALF, HALF), HALF)
        other_cols = pl.ds(pl.multiple_of((1 - half) * HALF, HALF), HALF)
        return (
            pltpu.make_async_copy(mine.at[w, :, own_cols], out_ref.at[w, own_rows, :], save_sem.at[0, w]),
            pltpu.make_async_copy(seen.at[w], s_ref.at[:, w, own_rows, :], save_sem.at[1, w]),
        ), (
            pltpu.make_async_remote_copy(
                src_ref=mine.at[w, :, other_cols], dst_ref=out_ref.at[w, own_rows, :],
                send_sem=pair_send.at[0, w], recv_sem=pair_recv.at[0, w],
                device_id=partner, device_id_type=MESH,
            ),
            pltpu.make_async_remote_copy(
                src_ref=seen.at[w], dst_ref=s_ref.at[:, w, own_rows, :],
                send_sem=pair_send.at[1, w], recv_sem=pair_recv.at[1, w],
                device_id=partner, device_id_type=MESH,
            ),
        )

    def wave(w, carry):
        def deep(k, sums):
            cs = pl.ds(pl.multiple_of(k * 1024, 1024), 1024)
            piece = jnp.concatenate([
                (
                    bulk[w, :, pl.ds(pl.multiple_of(k * 1024 + r * HEAD, HEAD), HEAD)].astype(F32)
                    * v_ref[0, pl.ds(k * 8 + r, 1), :]
                ).astype(BF16)
                for r in range(8)
            ], axis=1)
            return (
                sums[0] + jnp.dot(piece, full[0, cs, :], preferred_element_type=F32),
                sums[1] + jnp.dot(piece, full[1, cs, :], preferred_element_type=F32),
            )

        def from_bulk():
            bulk_copy(w, {"section": sec}).wait_recv()
            zero = jnp.zeros((ROWS, HALF), F32)
            return lax.fori_loop(0, 8, deep, (zero, zero))

        def from_start():
            return (start[0, w], start[1, w])

        sums = lax.cond(sec >= 4, from_bulk, from_start)
        for i in (2, 1, 0):
            def more(sums, i=i):
                near_copy(i, w, {"section": sec}).wait_recv()
                piece = near[i, w]
                return (
                    sums[0] + jnp.dot(piece, fold[0, i], preferred_element_type=F32),
                    sums[1] + jnp.dot(piece, fold[1, i], preferred_element_type=F32),
                )

            sums = lax.cond(sec > i, more, lambda sums: sums, sums)
        mine[w, :, :HALF] = sums[0].astype(BF16)
        mine[w, :, HALF:] = sums[1].astype(BF16)
        for i in range(3):
            @pl.when(sec + i + 1 < sections)
            def _():
                near_copy(i, w, {"section": sec + i + 1}).start()

        def assemble(c, carry):
            heads = pl.ds(pl.multiple_of(c * HEAD, HEAD), HEAD)
            y1 = near[0, w, :, heads].astype(F32) * root
            y2 = near[1, w, :, heads].astype(F32) * root
            y3 = near[2, w, :, heads].astype(F32) * root
            y0 = mine[w, :, heads].astype(F32) * root
            for r in range(8):
                cs = pl.ds(pl.multiple_of(c * 1024 + r * HEAD, HEAD), HEAD)
                row = pl.ds(c * 8 + r, 1)
                now = v_ref[0, row, :] * bulk[w, :, cs].astype(F32) + v_ref[1, row, :] * y3 + v_ref[2, row, :] * y2 + y1
                spot = pl.ds(pl.multiple_of(lax.rem(c, 2) * 1024 + r * HEAD, HEAD), HEAD)
                seen[w, lax.div(c, 2), :, spot] = now.astype(BF16)
                ahead[w, :, cs] = (v_ref[3, row, :] * now + y0).astype(BF16)
            return carry

        lax.fori_loop(0, 8, assemble, 0)

        @pl.when(sec + 4 < sections)
        def _():
            bulk_copy(w, {"section": sec + 4}).start()

        local, remote = tail_copies(w)
        for copy in remote + local:
            copy.start()
        return carry

    lax.fori_loop(0, MICRO, wave, 0)

    def finish(w, carry):
        for i in range(3):
            @pl.when(sec + i + 1 < sections)
            def _():
                near_copy(i, w, {"section": sec + i + 1}).wait_send()

        @pl.when(sec + 4 < sections)
        def _():
            bulk_copy(w, {"section": sec + 4}).wait_send()

        local, remote = tail_copies(w)
        for copy in local:
            copy.wait()
        for copy in remote:
            copy.wait()
        return carry

    lax.fori_loop(0, MICRO, finish, 0)

    @pl.when(sec < 1)
    def _():
        m_local.wait()
        m_other.wait()


def chain(inputs, quant, folds, first, vectors, after):
    anywhere = pl.BlockSpec(memory_space=pl.ANY)
    dma = pltpu.SemaphoreType.DMA
    return pl.pallas_call(
        chain_body,
        in_specs=[anywhere, anywhere, anywhere, anywhere, pl.BlockSpec(memory_space=pltpu.VMEM), anywhere],
        out_specs=[anywhere, anywhere],
        out_shape=[
            jax.ShapeDtypeStruct((MICRO, 32, HALF), BF16),
            jax.ShapeDtypeStruct((4, MICRO, 32, D // 4), BF16),
        ],
        scratch_shapes=[
            pltpu.VMEM((2, D, HALF), BF16),
            pltpu.VMEM((2, 3, KV, HALF), BF16),
            pltpu.VMEM((2, MICRO, ROWS, HALF), F32),
            pltpu.VMEM((MICRO, ROWS, D), BF16),
            pltpu.VMEM((MICRO, ROWS, D), BF16),
            pltpu.VMEM((MICRO, 4, ROWS, D // 4), BF16),
            pltpu.VMEM((3, MICRO, ROWS, KV), BF16),
            pltpu.VMEM((MICRO, ROWS, KV), BF16),
            dma((3,)),
            dma((3,)),
            dma((3,)),
            dma,
            dma((3, MICRO)),
            dma((3, MICRO)),
            dma((MICRO,)),
            dma((MICRO,)),
            dma((2, MICRO)),
            dma((2, MICRO)),
            dma((2, MICRO)),
        ],
        compiler_params=pltpu.CompilerParams(
            collective_id=0, has_side_effects=True, vmem_limit_bytes=60 * 1024 * 1024
        ),
        name="chain",
    )(inputs, quant, folds, first, vectors, after)


def local(inputs, value_weight, carry_gain, channel_bins, grid_picks):
    weight = value_weight[0]
    bins = channel_bins.reshape(D // 128, 128)
    gains = gains_of(carry_gain.reshape(D // 128, 128))
    quant, folds, first = first_pick(grid_picks, bins, gains, weight, inputs)
    delta = deltas(False, grid_picks, bins, weight, folds, quant)
    quant_out, stream = chain(inputs, quant, folds, first, gains, delta)
    delta = deltas(True, grid_picks, bins, weight, delta, stream)
    part = losses(stream.reshape(4, MICRO * 32, D // 4), delta)
    total = reduce_all(part)
    entry_count = inputs.shape[0] * inputs.shape[1] * lax.axis_size("dp") * KV
    grid_loss = jnp.sum(total[:PICKS], axis=1) * (LOSS_UNIT / entry_count)
    return (quant_out[None], grid_loss[None])


def solution(mesh):
    placed = (
        P(None, "dp", None),
        P("section", None, "mp"),
        P("section", None),
        P("section", None),
        P("section", None),
    )
    return jax.shard_map(
        local,
        mesh=mesh,
        in_specs=placed,
        out_specs=(P("section", None, "dp", "mp"), P("section", None)),
        check_vma=False,
    )
```

time: 284 us -> 230 us (0.81)
  the two profiles are of different devices: /device:TPU:121 before, /device:TPU:249 now
where the time goes in v2:
time: 230 us; the launch traced here: 229 us
  Pallas kernels  227 us (99%)
    pallas_call x1, Pallas kernels, chain(): pl.pallas_call(chain_body, in_specs=[anywhere, anywhere, anywhere, anywhe...  86.5 us
    pallas_call x2, Pallas kernels, deltas(): pl.pallas_call(functools.partial(deltas_body, later), in_specs=[pl.BlockS...  77.3 us
    pallas_call x1, Pallas kernels, first_pick(): pl.pallas_call(first_body, grid=(8,), in_specs=[pl.BlockSpec(memory_space...  29.5 us
    pallas_call x1, Pallas kernels, losses(): pl.pallas_call(losses_body, grid=(PICKS, parts), in_specs=[pl.BlockSpec((...  19.7 us
    pallas_call x1, Pallas kernels, reduce_all(): pl.pallas_call(reduce_body, in_specs=[pl.BlockSpec(memory_space=pltpu.VME...  7.08 us
    pallas_call x1, Pallas kernels, gains_of(): pl.pallas_call(gains_body, in_specs=[pl.BlockSpec(memory_space=pltpu.VMEM...  6.42 us

profile of v2, /device:TPU:249, one launch (start us, length us, event | category | flops | bytes accessed | tf_op | source)
XLA Modules:
  0.0 229.1 jit_solution(3707481419132239399)
XLA Ops:
  0.6 6.4 %gains.1.g_ref.v_ref = f32[4,64,128]{2,1,0:T(8,128)} custom-call(f32[64,128]{1,0:T(8,128)} %bitcast.15), custom_call_target="tpu_custom_call" | custom-call | tf_op jit(solution)/shard_map/gains/pallas_call | solution.py:323
  7.1 29.5 %first_pick.1 = (bf16[8192,512]{1,0:T(8,128)(2,1)}, bf16[3,1024,512]{2,1,0:T(8,128)(2,1)}, f32[4,32,512]{2,1,0:T(8,128)}) custom-call(s32[1,20]{1,0:T(1,128)} %picks_ref.5, s32[64,128]{1,0:T(8,128)} %bitcast.11, f32[4,64,128]{2,1,0:T(8,128)} %gains.1.g_ref.v_ref, bf16[8192,512]{1,0:T(8,128)(2,1)} %bitcast.7, bf16[4,32,8192]{2,1,0:T(8,128)(2,1)} %x_ref.3), custom_call_target="tpu_custom_call" | custom-call | tf_op jit(solution)/shard_map/first_pick/pallas_call | solution.py:117
  36.5 76.4 %deltas_before.1.after_ref.old_ref = bf16[4,8192,512]{2,1,0:T(8,128)(2,1)} custom-call(s32[1,20]{1,0:T(1,128)} %picks_ref.5, s32[64,128]{1,0:T(8,128)} %bitcast.12, bf16[8192,512]{1,0:T(8,128)(2,1)} %bitcast.8, bf16[3,1024,512]{2,1,0:T(8,128)(2,1)} %get-tuple-element.8.old_ref.m_ref, bf16[8192,512]{1,0:T(8,128)(2,1)} %get-tuple-element.7.after_ref.q_ref), custom_call_target="tpu_custom_call" | custom-call | tf_op jit(solution)/shard_map/deltas_before/pallas_call | solution.py:212
  113.0 86.5 %chain.1 = (bf16[4,32,512]{2,1,0:T(8,128)(2,1)}, bf16[4,4,32,2048]{3,2,1,0:T(8,128)(2,1)}) custom-call(bf16[4,32,8192]{2,1,0:T(8,128)(2,1)} %x_ref.3, bf16[8192,512]{1,0:T(8,128)(2,1)} %get-tuple-element.7.after_ref.q_ref, bf16[3,1024,512]{2,1,0:T(8,128)(2,1)} %get-tuple-element.8.old_ref.m_ref, f32[4,32,512]{2,1,0:T(8,128)} %get-tuple-element.9.a_ref, ...), custom_call_target="tpu_custom_call" | custom-call | tf_op jit(solution)/shard_map/chain/pallas_call | solution.py:594
  199.5 0.9 deltas_later.1.d_ref
  200.4 0.0 copy-start
  200.4 19.7 %losses.1.x_ref = f32[8,128]{1,0:T(8,128)} custom-call(bf16[4,128,2048]{2,1,0:T(8,128)(2,1)} %bitcast.10, bf16[4,8192,512]{2,1,0:T(8,128)(2,1)} %deltas_later.1.d_ref), custom_call_target="tpu_custom_call" | custom-call | tf_op jit(solution)/shard_map/losses/pallas_call | solution.py:258
  220.1 7.1 %reduce_all.1 = f32[8,128]{1,0:T(8,128)} custom-call(f32[8,128]{1,0:T(8,128)} %losses.1.x_ref), custom_call_target="tpu_custom_call" | custom-call | tf_op jit(solution)/shard_map/reduce_all/pallas_call | solution.py:373
  227.2 0.8 slice_reduce_fusion
  228.0 0.5 multiply_bitcast_fusion
  228.5 0.0 copy-done
  228.5 0.7 copy.10
Async XLA Ops:
  200.4 28.1 %copy-start = (bf16[4,32,512]{2,1,0:T(8,128)(2,1)S(1)}, bf16[4,32,512]{2,1,0:T(8,128)(2,1)}, u32[]{:S(2)}) copy-start(bf16[4,32,512]{2,1,0:T(8,128)(2,1)} %get-tuple-element.10) | copy-start | bytes 393220

commit v3 on v2

--- a/solution.py
+++ b/solution.py
@@ -17,7 +17,7 @@
 PICKS = 4
 MICRO = 4
 ROWS = 16
-BEFORE = (10, 15, 20, 25)
+BEFORE = (9, 14, 20, 25)
 
 EPS = 1e-06
 LOSS_UNIT = 1000.0
@@ -43,14 +43,27 @@
     return acc * r
 
 
-def high_of(w_ref, wide, r, start, cs):
+def high_of(w_ref, wide, r, cs):
     high = None
     for q in range(4):
-        part = w_ref[pl.ds(pl.multiple_of(start + 32 * q, 32), 32), cs].astype(F32)
-        part = jnp.abs(part * wide[r, pl.ds(32 * q, 32), :])
+        part = w_ref[r * GROUP + 32 * q : r * GROUP + 32 * q + 32, cs].astype(F32)
+        part = jnp.abs(part * wide[r, 32 * q : 32 * q + 32, :])
         part = jnp.max(part, axis=0, keepdims=True)
         high = part if high is None else jnp.maximum(high, part)
     return high + EPS
+
+
+def quantized(w_ref, wide, back, r, put):
+    for c in range(4):
+        cs = slice(c * 128, c * 128 + 128)
+        high = high_of(w_ref, wide, r, cs)
+        up = 7.0 / high
+        down = high * (-1.0 / 7.0)
+        for q in range(4):
+            rows = slice(32 * q, 32 * q + 32)
+            at = slice(r * GROUP + 32 * q, r * GROUP + 32 * q + 32)
+            w = w_ref[at, cs].astype(F32)
+            put(at, cs, rounding_part(w, wide[r, rows, :], back[r, rows, :], up, down).astype(BF16))
 
 
 def scales_of(bins, pick, wide, back):
@@ -66,54 +79,101 @@
     return sine_part(w * scale * up) * down * back
 
 
-def first_body(picks_ref, bins_ref, g_ref, w_ref, x_ref, q_ref, m_ref, a_ref, wide, back, left, acc):
+def first_body(
+    picks_ref, bins_ref, g_ref, w_ref, x_ref,
+    q_ref, m_ref, a_ref,
+    wide, back, near_gain, far_gain, left, acc, made, folds, first,
+    q_sem, m_sem, a_sem,
+):
     head = pl.program_id(0)
+    half = lax.axis_index("mp")
+    partner = {"mp": 1 - half}
+
+    def pieces(h):
+        at = pl.ds(pl.multiple_of(h * 1024, 1024), 1024)
+        src = made.at[h]
+        rows = pl.ds(pl.multiple_of(h * HEAD, HEAD), HEAD)
+        return (
+            pltpu.make_async_copy(src, q_ref.at[half, at, :], q_sem.at[0, h]),
+            pltpu.make_async_copy(folds.at[:, rows, :], m_ref.at[half, :, rows, :], m_sem.at[0, h]),
+            pltpu.make_async_remote_copy(
+                src_ref=folds.at[:, rows, :], dst_ref=m_ref.at[half, :, rows, :],
+                send_sem=m_sem.at[1, h], recv_sem=m_sem.at[2, h], device_id=partner, device_id_type=MESH,
+            ),
+            pltpu.make_async_remote_copy(
+                src_ref=src, dst_ref=q_ref.at[half, at, :],
+                send_sem=q_sem.at[1, h], recv_sem=q_sem.at[2, h], device_id=partner, device_id_type=MESH,
+            ),
+        )
+
+    @pl.when(head == 0)
+    def _():
+        barrier = pltpu.get_barrier_semaphore()
+        pl.semaphore_signal(barrier, inc=1, device_id=partner, device_id_type=MESH)
+        pl.semaphore_wait(barrier, 1)
+        acc[...] = jnp.zeros_like(acc)
+
     scales_of(bins_ref[...], picks_ref[0, 0], wide, back)
-    eye = lax.broadcasted_iota(jnp.int32, (HEAD, HEAD), 0) == lax.broadcasted_iota(jnp.int32, (HEAD, HEAD), 1)
+    near_columns, far_columns = g_ref[2].T, g_ref[1].T
     for r in range(8):
-        cs = pl.ds(r * HEAD, HEAD)
-        row = jnp.ones((1, HEAD), F32)
-        for i, gain in enumerate((row, g_ref[2, r : r + 1, :], g_ref[1, r : r + 1, :])):
-            left[i * HEAD : (i + 1) * HEAD, cs] = jnp.where(eye, gain, 0.0).astype(BF16)
+        near_gain[r] = jnp.broadcast_to(near_columns[:, r : r + 1], (GROUP, 128))
+        far_gain[r] = jnp.broadcast_to(far_columns[:, r : r + 1], (GROUP, 128))
+        cs = slice(r * HEAD, r * HEAD + HEAD)
         for w in range(MICRO):
-            left[384 + w * 32 : 416 + w * 32, cs] = (
-                x_ref[w, :, cs].astype(F32) * g_ref[0, r : r + 1, :]
-            ).astype(BF16)
-
-    def block(r, carry):
-        start = r * GROUP
-        for c in range(4):
-            cs = pl.ds(c * 128, 128)
-            high = high_of(w_ref, wide, r, start, cs)
-            up = 7.0 / high
-            down = high * (-1.0 / 7.0)
-            for q in range(4):
-                rows = pl.ds(32 * q, 32)
-                at = pl.ds(pl.multiple_of(start + 32 * q, 32), 32)
+            left[w * 32 : w * 32 + 32, cs] = (x_ref[w, :, cs].astype(F32) * g_ref[0, r : r + 1, :]).astype(BF16)
+
+    head_rows = pl.multiple_of(head * HEAD, HEAD)
+    root = 1.0 / math.sqrt(32.0)
+    for c in range(4):
+        cs = slice(c * 128, c * 128 + 128)
+        highs = [high_of(w_ref, wide, r, cs) for r in range(8)]
+        ups = [7.0 / high for high in highs]
+        downs = [high * (-1.0 / 7.0) for high in highs]
+        for q in range(4):
+            rows = slice(32 * q, 32 * q + 32)
+            sums = None
+            for r in range(8):
+                at = slice(r * GROUP + 32 * q, r * GROUP + 32 * q + 32)
                 w = w_ref[at, cs].astype(F32)
-                q_ref[at, cs] = (w + rounding_part(w, wide[r, rows, :], back[r, rows, :], up, down)).astype(BF16)
-        return carry
-
-    lax.fori_loop(0, 8, block, 0)
-    product = jnp.dot(left[...], q_ref[...], preferred_element_type=F32)
-    for i in range(3):
-        m_ref[i] = (product[i * HEAD : (i + 1) * HEAD] * (1.0 / math.sqrt(32.0))).astype(BF16)
-
-    @pl.when(head == 0)
-    def _():
-        acc[...] = product[384:]
-
-    @pl.when(head > 0)
-    def _():
-        acc[...] += product[384:]
+                value = w + rounding_part(w, wide[r, rows, :], back[r, rows, :], ups[r], downs[r])
+                made[head, at, cs] = value.astype(BF16)
+                terms = (value, value * near_gain[r, rows, :], value * far_gain[r, rows, :])
+                sums = terms if sums is None else tuple(x + y for x, y in zip(sums, terms))
+            for i in range(3):
+                folds[i, pl.ds(head_rows + 32 * q, 32), cs] = (sums[i] * root).astype(BF16)
+        if c % 2:
+            half_cols = slice(c * 128 - 128, c * 128 + 128)
+            acc[:, half_cols] += jnp.dot(left[...], made[head, :, half_cols], preferred_element_type=F32)
+    for copy in pieces(head):
+        copy.start()
 
     @pl.when(head == 7)
     def _():
-        for w in range(MICRO):
-            a_ref[w] = acc[w * 32 : w * 32 + 32]
+        for side in range(2):
+            for w in range(MICRO):
+                at = w * 32 + side * ROWS
+                first[side, w] = acc[at : at + ROWS, :]
+        local = pltpu.make_async_copy(first.at[half], a_ref.at[half], a_sem.at[0])
+        other = pltpu.make_async_remote_copy(
+            src_ref=first.at[1 - half], dst_ref=a_ref.at[half], send_sem=a_sem.at[1], recv_sem=a_sem.at[2],
+            device_id=partner, device_id_type=MESH,
+        )
+        other.start()
+        local.start()
+
+        def finish(h, carry):
+            for copy in pieces(h):
+                copy.wait()
+            return carry
+
+        lax.fori_loop(0, 8, finish, 0)
+        local.wait()
+        other.wait()
 
 
 def first_pick(picks, bins, gains, weight, inputs):
+    anywhere = pl.BlockSpec(memory_space=pl.ANY)
+    dma = pltpu.SemaphoreType.DMA
     return pl.pallas_call(
         first_body,
         grid=(8,),
@@ -124,113 +184,116 @@
             pl.BlockSpec((1024, HALF), lambda h: (h, 0)),
             pl.BlockSpec((MICRO, 32, 1024), lambda h: (0, 0, h)),
         ],
-        out_specs=[
-            pl.BlockSpec((1024, HALF), lambda h: (h, 0)),
-            pl.BlockSpec((3, HEAD, HALF), lambda h: (0, h, 0)),
-            pl.BlockSpec((MICRO, 32, HALF), lambda h: (0, 0, 0)),
-        ],
+        out_specs=[anywhere, anywhere, anywhere],
         out_shape=[
-            jax.ShapeDtypeStruct((D, HALF), BF16),
-            jax.ShapeDtypeStruct((3, KV, HALF), BF16),
-            jax.ShapeDtypeStruct((MICRO, 32, HALF), F32),
+            jax.ShapeDtypeStruct((2, D, HALF), BF16),
+            jax.ShapeDtypeStruct((2, 3, KV, HALF), BF16),
+            jax.ShapeDtypeStruct((2, MICRO, ROWS, HALF), F32),
         ],
         scratch_shapes=[
             pltpu.VMEM((8, GROUP, 128), F32),
             pltpu.VMEM((8, GROUP, 128), F32),
-            pltpu.VMEM((512, 1024), BF16),
+            pltpu.VMEM((8, GROUP, 128), F32),
+            pltpu.VMEM((8, GROUP, 128), F32),
+            pltpu.VMEM((128, 1024), BF16),
             pltpu.VMEM((128, HALF), F32),
-        ],
+            pltpu.VMEM((8, 1024, HALF), BF16),
+            pltpu.VMEM((3, KV, HALF), BF16),
+            pltpu.VMEM((2, MICRO, ROWS, HALF), F32),
+            dma((3, 8)),
+            dma((3, 8)),
+            dma((3,)),
+        ],
+        compiler_params=pltpu.CompilerParams(collective_id=3, has_side_effects=True),
         name="first_pick",
     )(picks, bins, gains, weight, inputs)
 
 
-def picks_before(sec):
-    return sum(jnp.where(sec >= least, 1, 0) for least in BEFORE)
-
-
-def deltas_body(later, picks_ref, bins_ref, w_ref, old_ref, after_ref, d_ref, held, made, wide, back, w_sem, d_sem):
-    split = picks_before(lax.axis_index("section"))
-    low, count = (split, (PICKS - split) * 8) if later else (0, split * 8)
-
-    def fetch(h):
-        at = pl.ds(pl.multiple_of(h * 1024, 1024), 1024)
-        return pltpu.make_async_copy(w_ref.at[at, :], held.at[at, :], w_sem.at[h])
-
-    def put(t):
-        at = pl.ds(pl.multiple_of(lax.rem(t, 8) * 1024, 1024), 1024)
-        slot = lax.rem(t, 2)
-        return pltpu.make_async_copy(made.at[slot], d_ref.at[low + lax.div(t, 8), at, :], d_sem.at[slot])
-
-    @pl.when(count > 0)
-    def _():
-        for h in range(8):
-            fetch(h).start()
-
-    def step(t, carry):
-        h = lax.rem(t, 8)
-        slot = lax.rem(t, 2)
-
-        @pl.when(t < 8)
-        def _():
-            fetch(h).wait()
-
-        @pl.when(t >= 2)
-        def _():
-            put(t - 2).wait()
-
-        scales_of(bins_ref[pl.ds(pl.multiple_of(h * 8, 8), 8), :], picks_ref[0, low + lax.div(t, 8)], wide, back)
-
-        def block(r, carry):
-            start = h * 1024 + r * GROUP
-            for c in range(4):
-                cs = pl.ds(c * 128, 128)
-                high = high_of(held, wide, r, start, cs)
-                up = 7.0 / high
-                down = high * (-1.0 / 7.0)
-                for q in range(4):
-                    rows = pl.ds(32 * q, 32)
-                    w = held[pl.ds(pl.multiple_of(start + 32 * q, 32), 32), cs].astype(F32)
-                    made[slot, pl.ds(pl.multiple_of(r * GROUP + 32 * q, 32), 32), cs] = rounding_part(
-                        w, wide[r, rows, :], back[r, rows, :], up, down
-                    ).astype(BF16)
-            return carry
-
-        lax.fori_loop(0, 8, block, 0)
-        put(t).start()
-        return carry
-
-    lax.fori_loop(0, count, step, 0)
-
-    @pl.when(count > 0)
-    def _():
-        put(count - 2).wait()
-        put(count - 1).wait()
-
-
-def deltas(later, picks, bins, weight, old, after):
-    anywhere = pl.BlockSpec(memory_space=pl.ANY)
+def deltas_body(picks_ref, bins_ref, w_ref, after_ref, d_ref, wide, back):
+    scales_of(bins_ref[...], picks_ref[0, pl.program_id(0)], wide, back)
+
+    def put(rows, columns, value):
+        d_ref[0, rows, columns] = value
+
+    for r in range(8):
+        quantized(w_ref, wide, back, r, put)
+
+
+def deltas(count, picks, bins, weight, after):
     return pl.pallas_call(
-        functools.partial(deltas_body, later),
+        deltas_body,
+        grid=(count, 8),
         in_specs=[
             pl.BlockSpec(memory_space=pltpu.SMEM),
-            pl.BlockSpec(memory_space=pltpu.VMEM),
-            anywhere,
-            anywhere,
-            anywhere,
-        ],
-        out_specs=anywhere,
+            pl.BlockSpec((8, 128), lambda p, h: (h, 0)),
+            pl.BlockSpec((1024, HALF), lambda p, h: (h, 0)),
+            pl.BlockSpec(memory_space=pl.ANY),
+        ],
+        out_specs=pl.BlockSpec((1, 1024, HALF), lambda p, h: (p, h, 0)),
         out_shape=jax.ShapeDtypeStruct((PICKS, D, HALF), BF16),
-        input_output_aliases={3: 0} if later else {},
+        scratch_shapes=[pltpu.VMEM((8, GROUP, 128), F32), pltpu.VMEM((8, GROUP, 128), F32)],
+        name="deltas",
+    )(picks, bins, weight, after)
+
+
+def nothing(weight):
+    return pl.pallas_call(
+        lambda w_ref, d_ref: None,
+        in_specs=[pl.BlockSpec(memory_space=pl.ANY)],
+        out_specs=pl.BlockSpec(memory_space=pl.ANY),
+        out_shape=jax.ShapeDtypeStruct((PICKS, D, HALF), BF16),
+        name="nothing",
+    )(weight)
+
+
+def squares(acc):
+    total = jnp.sum(jnp.square(acc), axis=0, keepdims=True)
+    return total[:, :128] + total[:, 128:256] + total[:, 256:384] + total[:, 384:]
+
+
+def fused_body(low, picks_ref, bins_ref, w_ref, s_ref, o_ref, wide, back, made, acc):
+    pick = low + pl.program_id(0)
+    head = pl.program_id(1)
+    scales_of(bins_ref[...], picks_ref[0, pick], wide, back)
+
+    @pl.when(head == 0)
+    def _():
+        acc[...] = jnp.zeros_like(acc)
+
+    def put(rows, columns, value):
+        made[rows, columns] = value
+
+    for part in range(2):
+        for r in range(4):
+            quantized(w_ref, wide, back, part * 4 + r, put)
+        rows = slice(part * 512, part * 512 + 512)
+        acc[...] += jnp.dot(s_ref[0, :, rows], made[rows, :], preferred_element_type=F32)
+
+    @pl.when(head == 7)
+    def _():
+        o_ref[pl.ds(pick, 1), :] = squares(acc[...])
+
+
+def fused(low, picks, bins, weight, stream):
+    return pl.pallas_call(
+        functools.partial(fused_body, low),
+        grid=(PICKS - low, 8),
+        in_specs=[
+            pl.BlockSpec(memory_space=pltpu.SMEM),
+            pl.BlockSpec((8, 128), lambda p, h: (h, 0)),
+            pl.BlockSpec((1024, HALF), lambda p, h: (h, 0)),
+            pl.BlockSpec((1, 128, 1024), lambda p, h: (lax.div(h, 2), 0, lax.rem(h, 2))),
+        ],
+        out_specs=pl.BlockSpec((8, 128), lambda p, h: (0, 0)),
+        out_shape=jax.ShapeDtypeStruct((8, 128), F32),
         scratch_shapes=[
-            pltpu.VMEM((D, HALF), BF16),
-            pltpu.VMEM((2, 1024, HALF), BF16),
             pltpu.VMEM((8, GROUP, 128), F32),
             pltpu.VMEM((8, GROUP, 128), F32),
-            pltpu.SemaphoreType.DMA((8,)),
-            pltpu.SemaphoreType.DMA((2,)),
-        ],
-        name="deltas_later" if later else "deltas_before",
-    )(picks, bins, weight, old, after)
+            pltpu.VMEM((1024, HALF), BF16),
+            pltpu.VMEM((128, HALF), F32),
+        ],
+        name="fused",
+    )(picks, bins, weight, stream)
 
 
 def losses_body(s_ref, d_ref, o_ref, acc):
@@ -247,17 +310,15 @@
 
     @pl.when(part == pl.num_programs(1) - 1)
     def _():
-        total = jnp.sum(jnp.square(acc[...]), axis=0, keepdims=True)
-        total = total[:, :128] + total[:, 128:256] + total[:, 256:384] + total[:, 384:]
-        o_ref[pl.ds(pl.program_id(0), 1), :] = total
-
-
-def losses(stream, delta):
+        o_ref[pl.ds(pl.program_id(0), 1), :] = squares(acc[...])
+
+
+def losses(count, stream, delta):
     depth = 2048
     parts = D // depth
     return pl.pallas_call(
         losses_body,
-        grid=(PICKS, parts),
+        grid=(count, parts),
         in_specs=[
             pl.BlockSpec((parts, 128, depth), lambda p, k: (0, 0, 0)),
             pl.BlockSpec((1, depth, HALF), lambda p, k: (p, k, 0)),
@@ -389,7 +450,7 @@
     x_ref, q_ref, m_ref, a_ref, v_ref, after_ref,
     out_ref, s_ref,
     full, fold, start, bulk, ahead, seen, near, mine,
-    q_sem, m_sem, a_sem, x_sem, near_send, near_recv, bulk_send, bulk_recv, save_sem, pair_send, pair_recv,
+    q_sem, m_sem, a_sem, x_sem, next_send, next_recv, near_send, near_recv, bulk_send, bulk_recv, save_sem, pair_send, pair_recv,
 ):
     sections = lax.axis_size("section")
     sec = lax.axis_index("section")
@@ -402,6 +463,23 @@
         def _():
             near[i] = jnp.zeros_like(near.at[i])
 
+    own_rows = pl.ds(pl.multiple_of(half * ROWS, ROWS), ROWS)
+    x_copy = pltpu.make_async_copy(x_ref.at[:, own_rows, :], bulk, x_sem)
+    a_copy = pltpu.make_async_copy(a_ref, start, a_sem)
+    m_copy = pltpu.make_async_copy(m_ref, fold, m_sem)
+    q_copy = pltpu.make_async_copy(q_ref, full, q_sem)
+    a_copy.start()
+
+    @pl.when(sec < 4)
+    def _():
+        x_copy.start()
+
+    m_copy.start()
+
+    @pl.when(sec >= 4)
+    def _():
+        q_copy.start()
+
     barrier = pltpu.get_barrier_semaphore()
     pl.semaphore_signal(barrier, inc=1, device_id=partner, device_id_type=MESH)
     count = jnp.int32(1)
@@ -417,51 +495,24 @@
         count = count + jnp.where(sec + step < sections, 1, 0) + jnp.where(sec >= step, 1, 0)
     pl.semaphore_wait(barrier, count)
 
-    q_local = pltpu.make_async_copy(q_ref, full.at[half], q_sem.at[0])
-    q_other = pltpu.make_async_remote_copy(
-        src_ref=q_ref, dst_ref=full.at[half], send_sem=q_sem.at[1], recv_sem=q_sem.at[2],
-        device_id=partner, device_id_type=MESH,
-    )
-    m_local = pltpu.make_async_copy(m_ref, fold.at[half], m_sem.at[0])
-    m_other = pltpu.make_async_remote_copy(
-        src_ref=m_ref, dst_ref=fold.at[half], send_sem=m_sem.at[1], recv_sem=m_sem.at[2],
-        device_id=partner, device_id_type=MESH,
-    )
-    own_rows = pl.ds(pl.multiple_of(half * ROWS, ROWS), ROWS)
-    other_rows = pl.ds(pl.multiple_of((1 - half) * ROWS, ROWS), ROWS)
-    a_local = pltpu.make_async_copy(a_ref.at[:, own_rows, :], start.at[half], a_sem.at[0])
-    a_other = pltpu.make_async_remote_copy(
-        src_ref=a_ref.at[:, other_rows, :], dst_ref=start.at[half], send_sem=a_sem.at[1], recv_sem=a_sem.at[2],
-        device_id=partner, device_id_type=MESH,
-    )
-    x_copy = pltpu.make_async_copy(x_ref.at[:, own_rows, :], bulk, x_sem)
-    a_other.start()
-    m_other.start()
-    a_local.start()
-    m_local.start()
+    a_copy.wait()
 
     @pl.when(sec < 4)
     def _():
-        x_copy.start()
         x_copy.wait()
 
+    m_copy.wait()
+
     @pl.when(sec >= 4)
     def _():
-        q_other.start()
-        q_local.start()
-
-    a_local.wait()
-    a_other.wait()
-
-    @pl.when(sec >= 1)
-    def _():
-        m_local.wait()
-        m_other.wait()
-
-    @pl.when(sec >= 4)
-    def _():
-        q_local.wait()
-        q_other.wait()
+        q_copy.wait()
+
+    def next_copy(part, w, target):
+        cols = slice(part * HALF, part * HALF + HALF)
+        return pltpu.make_async_remote_copy(
+            src_ref=mine.at[w, :, cols], dst_ref=near.at[0, w, :, cols], send_sem=next_send.at[part, w],
+            recv_sem=next_recv.at[part, w], device_id=target, device_id_type=MESH,
+        )
 
     def near_copy(i, w, target):
         return pltpu.make_async_remote_copy(
@@ -518,7 +569,7 @@
             return (start[0, w], start[1, w])
 
         sums = lax.cond(sec >= 4, from_bulk, from_start)
-        for i in (2, 1, 0):
+        for i in (2, 1):
             def more(sums, i=i):
                 near_copy(i, w, {"section": sec}).wait_recv()
                 piece = near[i, w]
@@ -528,9 +579,36 @@
                 )
 
             sums = lax.cond(sec > i, more, lambda sums: sums, sums)
-        mine[w, :, :HALF] = sums[0].astype(BF16)
-        mine[w, :, HALF:] = sums[1].astype(BF16)
-        for i in range(3):
+
+        def send(part, value):
+            mine[w, :, part * HALF : part * HALF + HALF] = value.astype(BF16)
+
+            @pl.when(sec + 1 < sections)
+            def _():
+                next_copy(part, w, {"section": sec + 1}).start()
+
+        def last(sums):
+            next_copy(0, w, {"section": sec}).wait_recv()
+            piece = near[0, w, :, :HALF]
+            sums = (
+                sums[0] + jnp.dot(piece, fold[0, 0, :HALF, :], preferred_element_type=F32),
+                sums[1] + jnp.dot(piece, fold[1, 0, :HALF, :], preferred_element_type=F32),
+            )
+            next_copy(1, w, {"section": sec}).wait_recv()
+            piece = near[0, w, :, HALF:]
+            send(0, sums[0] + jnp.dot(piece, fold[0, 0, HALF:, :], preferred_element_type=F32))
+            send(1, sums[1] + jnp.dot(piece, fold[1, 0, HALF:, :], preferred_element_type=F32))
+
+        @pl.when(sec > 0)
+        def _():
+            last(sums)
+
+        @pl.when(sec == 0)
+        def _():
+            send(0, sums[0])
+            send(1, sums[1])
+
+        for i in (1, 2):
             @pl.when(sec + i + 1 < sections)
             def _():
                 near_copy(i, w, {"section": sec + i + 1}).start()
@@ -564,7 +642,12 @@
     lax.fori_loop(0, MICRO, wave, 0)
 
     def finish(w, carry):
-        for i in range(3):
+        @pl.when(sec + 1 < sections)
+        def _():
+            next_copy(0, w, {"section": sec + 1}).wait_send()
+            next_copy(1, w, {"section": sec + 1}).wait_send()
+
+        for i in (1, 2):
             @pl.when(sec + i + 1 < sections)
             def _():
                 near_copy(i, w, {"section": sec + i + 1}).wait_send()
@@ -581,12 +664,6 @@
         return carry
 
     lax.fori_loop(0, MICRO, finish, 0)
-
-    @pl.when(sec < 1)
-    def _():
-        m_local.wait()
-        m_other.wait()
-
 
 def chain(inputs, quant, folds, first, vectors, after):
     anywhere = pl.BlockSpec(memory_space=pl.ANY)
@@ -608,10 +685,12 @@
             pltpu.VMEM((MICRO, 4, ROWS, D // 4), BF16),
             pltpu.VMEM((3, MICRO, ROWS, KV), BF16),
             pltpu.VMEM((MICRO, ROWS, KV), BF16),
-            dma((3,)),
-            dma((3,)),
-            dma((3,)),
             dma,
+            dma,
+            dma,
+            dma,
+            dma((2, MICRO)),
+            dma((2, MICRO)),
             dma((3, MICRO)),
             dma((3, MICRO)),
             dma((MICRO,)),
@@ -628,14 +707,31 @@
 
 
 def local(inputs, value_weight, carry_gain, channel_bins, grid_picks):
+    sec = lax.axis_index("section")
     weight = value_weight[0]
     bins = channel_bins.reshape(D // 128, 128)
     gains = gains_of(carry_gain.reshape(D // 128, 128))
     quant, folds, first = first_pick(grid_picks, bins, gains, weight, inputs)
-    delta = deltas(False, grid_picks, bins, weight, folds, quant)
+    count = sum(jnp.where(sec >= least, 1, 0) for least in BEFORE).astype(jnp.int32)
+    counts = range(PICKS + 1)
+    delta = lax.switch(count, [
+        functools.partial(deltas, n, grid_picks, bins, weight, first) if n else lambda: nothing(first)
+        for n in counts
+    ])
     quant_out, stream = chain(inputs, quant, folds, first, gains, delta)
-    delta = deltas(True, grid_picks, bins, weight, delta, stream)
-    part = losses(stream.reshape(4, MICRO * 32, D // 4), delta)
+    stream = stream.reshape(4, MICRO * 32, D // 4)
+    blank = jnp.zeros((8, 128), F32)
+    before, later = lax.switch(count, [
+        functools.partial(
+            lambda n: (
+                losses(n, stream, delta) if n else blank,
+                fused(n, grid_picks, bins, weight, stream) if n < PICKS else blank,
+            ),
+            n,
+        )
+        for n in counts
+    ])
+    part = jnp.where(jnp.arange(8)[:, None] < count, before, later)
     total = reduce_all(part)
     entry_count = inputs.shape[0] * inputs.shape[1] * lax.axis_size("dp") * KV
     grid_loss = jnp.sum(total[:PICKS], axis=1) * (LOSS_UNIT / entry_count)

time: 230 us -> 205 us (0.89)
  Pallas kernels: 227 us -> 201 us
    pallas_call x1, Pallas kernels: 86.5 us -> 71.4 us  [chain(): pl.pallas_call(chain_body, in_specs=[anywhere, anywhere, anywhere, anywhe...]
    pallas_call x3 -> x2, Pallas kernels: 97 us -> 85.3 us  [the longest x1 66.9 us: deltas(): pl.pallas_call(deltas_body, grid=(count, 8), in_specs=[pl.BlockSpec(memor...]
where the time goes in v3:
time: 205 us; the launch traced here: 204 us
  Pallas kernels  201 us (98%)
    pallas_call x1, Pallas kernels, chain(): pl.pallas_call(chain_body, in_specs=[anywhere, anywhere, anywhere, anywhe...  71.4 us
    pallas_call x1, Pallas kernels, deltas(): pl.pallas_call(deltas_body, grid=(count, 8), in_specs=[pl.BlockSpec(memor...  66.9 us
    pallas_call x1, Pallas kernels, first_pick(): pl.pallas_call(first_body, grid=(8,), in_specs=[pl.BlockSpec(memory_space...  30.7 us
    pallas_call x1, Pallas kernels, losses(): pl.pallas_call(losses_body, grid=(count, parts), in_specs=[pl.BlockSpec((...  18.4 us
    pallas_call x1, Pallas kernels, reduce_all(): pl.pallas_call(reduce_body, in_specs=[pl.BlockSpec(memory_space=pltpu.VME...  7.07 us
    pallas_call x1, Pallas kernels, gains_of(): pl.pallas_call(gains_body, in_specs=[pl.BlockSpec(memory_space=pltpu.VMEM...  6.43 us

profile of v3, /device:TPU:249, one launch (start us, length us, event | category | flops | bytes accessed | tf_op | source)
XLA Modules:
  0.0 204.4 jit_solution(5043995535733627154)
XLA Ops:
  0.7 6.4 %gains.1.g_ref.v_ref = f32[4,64,128]{2,1,0:T(8,128)} custom-call(f32[64,128]{1,0:T(8,128)} %bitcast.31), custom_call_target="tpu_custom_call" | custom-call | tf_op jit(solution)/shard_map/gains/pallas_call | solution.py:384
  7.1 30.7 %first_pick.1 = (bf16[2,8192,512]{2,1,0:T(8,128)(2,1)}, bf16[2,3,1024,512]{3,2,1,0:T(8,128)(2,1)}, f32[2,4,16,512]{3,2,1,0:T(8,128)S(1)}) custom-call(s32[1,20]{1,0:T(1,128)} %picks_ref.1, s32[64,128]{1,0:T(8,128)} %bitcast.21, f32[4,64,128]{2,1,0:T(8,128)} %gains.1.g_ref.v_ref, bf16[8192,512]{1,0:T(8,128)(2,1)} %bitcast.7, bf16[4,32,8192]{2,1,0:T(8,128)(2,1)} %x_ref.3), custom_call_target="tpu_custom_call" | custom-call | tf_op jit(solution)/shard_map/first_pick/pallas_call | solution.py:177
  37.8 66.9 %conditional.2 = (bf16[4,8192,512]{2,1,0:T(8,128)(2,1)}) conditional(s32[]{:T(128)} %clamp.4, f32[2,4,16,512]{3,2,1,0:T(8,128)S(1)} %get-tuple-element.129.a_ref, (s32[1,20]{1,0:T(1,128)}, s32[64,128]{1,0:T(8,128)}, bf16[8192,512]{1,0:T(8,128)(2,1)}, f32[2,4,16,512]{3,2,1,0:T(8,128)S(1)}) %tuple.73, ...), branch_computations={%region_0.1_spmd, %region_1.2_spmd, %region_2.3_spmd, %region_3.4_... | conditional | bytes 8 | solution.py:717
  37.8 66.9 %deltas.7 = bf16[4,8192,512]{2,1,0:T(8,128)(2,1)} custom-call(s32[1,20]{1,0:T(1,128)} %get-tuple-element.93.picks_ref, s32[64,128]{1,0:T(8,128)} %get-tuple-element.94.bins_ref, bf16[8192,512]{1,0:T(8,128)(2,1)} %get-tuple-element.95.w_ref, f32[2,4,16,512]{3,2,1,0:T(8,128)S(1)} %get-tuple-element.96.after_ref), custom_call_target="tpu_custom_call" | custom-call | tf_op jit(solution)/shard_map/cond/branch_4_fun/deltas/pallas_call | solution.py:223
  104.7 0.0 copy-start
  104.7 0.0 copy-start.2
  104.7 71.4 %chain.1 = (bf16[4,32,512]{2,1,0:T(8,128)(2,1)}, bf16[4,4,32,2048]{3,2,1,0:T(8,128)(2,1)S(1)}) custom-call(bf16[4,32,8192]{2,1,0:T(8,128)(2,1)} %x_ref.3, bf16[2,8192,512]{2,1,0:T(8,128)(2,1)} %get-tuple-element.127.q_ref, bf16[2,3,1024,512]{3,2,1,0:T(8,128)(2,1)} %get-tuple-element.128.m_ref, f32[2,4,16,512]{3,2,1,0:T(8,128)S(1)} %get-tuple-element.129.a_ref, ...), custom_call_target="tpu_custom_call" | custom-call | tf_op jit(solution)/shard_map/chain/pallas_call | solution.py:671
  176.1 0.0 copy-done
  176.1 0.0 copy-done.2
  176.2 0.0 copy-start.1
  176.2 18.5 %conditional.3 = (f32[8,128]{1,0:T(8,128)S(1)}, f32[8,128]{1,0:T(8,128)S(1)}) conditional(s32[]{:T(128)} %clamp.4, (s32[1,20]{1,0:T(1,128)S(1)}, s32[64,128]{1,0:T(8,128)S(1)}, bf16[8192,512]{1,0:T(8,128)(2,1)}, bf16[4,128,2048]{2,1,0:T(8,128)(2,1)S(1)}) %tuple.81, (bf16[4,128,2048]{2,1,0:T(8,128)(2,1)S(1)}, ...), branch_computations={%region_5.6_spmd, %region_6.7_spmd, %region_7.8_spmd, %region_8.9_... | conditional | bytes 4116 | solution.py:724
  176.2 18.4 %losses.7 = f32[8,128]{1,0:T(8,128)S(1)} custom-call(bf16[4,128,2048]{2,1,0:T(8,128)(2,1)S(1)} %get-tuple-element.116.s_ref, bf16[4,8192,512]{2,1,0:T(8,128)(2,1)} %get-tuple-element.117.d_ref), custom_call_target="tpu_custom_call" | custom-call | tf_op jit(solution)/shard_map/cond/branch_4_fun/losses/pallas_call | solution.py:319
  194.7 0.7 broadcast_select_fusion.x_ref
  195.3 7.1 %reduce_all.1 = f32[8,128]{1,0:T(8,128)} custom-call(f32[8,128]{1,0:T(8,128)} %broadcast_select_fusion.x_ref), custom_call_target="tpu_custom_call" | custom-call | tf_op jit(solution)/shard_map/reduce_all/pallas_call | solution.py:434
  202.4 0.8 slice_reduce_fusion
  203.2 0.5 multiply_bitcast_fusion
  203.7 0.0 copy-done.1
  203.7 0.7 copy.23
  (2 shorter events, 0.0 us)
Async XLA Ops:
  104.7 71.4 %copy-start = (s32[1,8192]{1,0:T(1,128)S(1)}, s32[1,8192]{1,0:T(1,128)}, u32[]{:S(2)}) copy-start(s32[1,8192]{1,0:T(1,128)} %param.18) | copy-start | bytes 98308
  104.7 71.4 %copy-start.2 = (s32[1,20]{1,0:T(1,128)S(1)}, s32[1,20]{1,0:T(1,128)}, u32[]{:S(2)}) copy-start(s32[1,20]{1,0:T(1,128)} %picks_ref.1) | copy-start | bytes 244
  176.2 27.6 %copy-start.1 = (bf16[4,32,512]{2,1,0:T(8,128)(2,1)S(1)}, bf16[4,32,512]{2,1,0:T(8,128)(2,1)}, u32[]{:S(2)}) copy-start(bf16[4,32,512]{2,1,0:T(8,128)(2,1)} %get-tuple-element.130) | copy-start | bytes 393220

commit v4 on v3

--- a/solution.py
+++ b/solution.py
@@ -209,8 +209,8 @@
     )(picks, bins, gains, weight, inputs)
 
 
-def deltas_body(picks_ref, bins_ref, w_ref, after_ref, d_ref, wide, back):
-    scales_of(bins_ref[...], picks_ref[0, pl.program_id(0)], wide, back)
+def deltas_body(low, picks_ref, bins_ref, w_ref, after_ref, d_ref, wide, back):
+    scales_of(bins_ref[...], picks_ref[0, low + pl.program_id(0)], wide, back)
 
     def put(rows, columns, value):
         d_ref[0, rows, columns] = value
@@ -219,9 +219,9 @@
         quantized(w_ref, wide, back, r, put)
 
 
-def deltas(count, picks, bins, weight, after):
+def deltas(low, count, picks, bins, weight, after):
     return pl.pallas_call(
-        deltas_body,
+        functools.partial(deltas_body, low),
         grid=(count, 8),
         in_specs=[
             pl.BlockSpec(memory_space=pltpu.SMEM),
@@ -251,83 +251,40 @@
     return total[:, :128] + total[:, 128:256] + total[:, 256:384] + total[:, 384:]
 
 
-def fused_body(low, picks_ref, bins_ref, w_ref, s_ref, o_ref, wide, back, made, acc):
-    pick = low + pl.program_id(0)
-    head = pl.program_id(1)
-    scales_of(bins_ref[...], picks_ref[0, pick], wide, back)
-
-    @pl.when(head == 0)
-    def _():
-        acc[...] = jnp.zeros_like(acc)
-
-    def put(rows, columns, value):
-        made[rows, columns] = value
-
-    for part in range(2):
-        for r in range(4):
-            quantized(w_ref, wide, back, part * 4 + r, put)
-        rows = slice(part * 512, part * 512 + 512)
-        acc[...] += jnp.dot(s_ref[0, :, rows], made[rows, :], preferred_element_type=F32)
-
-    @pl.when(head == 7)
-    def _():
-        o_ref[pl.ds(pick, 1), :] = squares(acc[...])
-
-
-def fused(low, picks, bins, weight, stream):
-    return pl.pallas_call(
-        functools.partial(fused_body, low),
-        grid=(PICKS - low, 8),
-        in_specs=[
-            pl.BlockSpec(memory_space=pltpu.SMEM),
-            pl.BlockSpec((8, 128), lambda p, h: (h, 0)),
-            pl.BlockSpec((1024, HALF), lambda p, h: (h, 0)),
-            pl.BlockSpec((1, 128, 1024), lambda p, h: (lax.div(h, 2), 0, lax.rem(h, 2))),
-        ],
-        out_specs=pl.BlockSpec((8, 128), lambda p, h: (0, 0)),
-        out_shape=jax.ShapeDtypeStruct((8, 128), F32),
-        scratch_shapes=[
-            pltpu.VMEM((8, GROUP, 128), F32),
-            pltpu.VMEM((8, GROUP, 128), F32),
-            pltpu.VMEM((1024, HALF), BF16),
-            pltpu.VMEM((128, HALF), F32),
-        ],
-        name="fused",
-    )(picks, bins, weight, stream)
-
-
-def losses_body(s_ref, d_ref, o_ref, acc):
-    part = pl.program_id(1)
-    product = jnp.dot(s_ref[part], d_ref[0], preferred_element_type=F32)
-
-    @pl.when(part == 0)
+def losses_body(s_ref, *refs):
+    *d_refs, o_ref, acc = refs
+    half = pl.program_id(1)
+    product = sum(
+        jnp.dot(
+            s_ref[2 * half + k // 2, :, (k % 2) * 1024 : (k % 2) * 1024 + 1024],
+            d_refs[k][0],
+            preferred_element_type=F32,
+        )
+        for k in range(4)
+    )
+
+    @pl.when(half == 0)
     def _():
         acc[...] = product
 
-    @pl.when(part > 0)
+    @pl.when(half == 1)
     def _():
-        acc[...] += product
-
-    @pl.when(part == pl.num_programs(1) - 1)
-    def _():
-        o_ref[pl.ds(pl.program_id(0), 1), :] = squares(acc[...])
+        o_ref[pl.ds(pl.program_id(0), 1), :] = squares(acc[...] + product)
 
 
 def losses(count, stream, delta):
-    depth = 2048
-    parts = D // depth
+    def piece(k):
+        return pl.BlockSpec((1, 1024, HALF), lambda p, h: (p, h * 4 + k, 0))
+
     return pl.pallas_call(
         losses_body,
-        grid=(count, parts),
-        in_specs=[
-            pl.BlockSpec((parts, 128, depth), lambda p, k: (0, 0, 0)),
-            pl.BlockSpec((1, depth, HALF), lambda p, k: (p, k, 0)),
-        ],
-        out_specs=pl.BlockSpec((8, 128), lambda p, k: (0, 0)),
+        grid=(count, 2),
+        in_specs=[pl.BlockSpec((4, 128, 2048), lambda p, h: (0, 0, 0)), *(piece(k) for k in range(4))],
+        out_specs=pl.BlockSpec((8, 128), lambda p, h: (0, 0)),
         out_shape=jax.ShapeDtypeStruct((8, 128), F32),
         scratch_shapes=[pltpu.VMEM((128, HALF), F32)],
         name="losses",
-    )(stream, delta)
+    )(stream, delta, delta, delta, delta)
 
 
 def gains_body(own_ref, o_ref, got, send_sem, recv_sem):
@@ -396,7 +353,7 @@
     )(own)
 
 
-def reduce_body(x_ref, o_ref, slots, send_sem, recv_sem):
+def reduce_body(unit, x_ref, o_ref, slots, send_sem, recv_sem):
     dp, mp = lax.axis_size("dp"), lax.axis_size("mp")
     peers = dp * mp
     rank = lax.axis_index("dp") * mp + lax.axis_index("mp")
@@ -424,18 +381,19 @@
         copies.append(copy)
     for copy in copies:
         copy.wait()
-    total = jnp.zeros_like(o_ref)
+    total = jnp.zeros_like(x_ref)
     for source in range(peers):
         total = total + slots[lax.rem(rank - source + peers, peers)]
-    o_ref[...] = total
-
-
-def reduce_all(part):
+    total = jnp.sum(total, axis=1, keepdims=True) * unit
+    o_ref[...] = jnp.broadcast_to(total, (8, 128)).T[0:1, 0:PICKS]
+
+
+def reduce_all(unit, part):
     return pl.pallas_call(
-        reduce_body,
+        functools.partial(reduce_body, unit),
         in_specs=[pl.BlockSpec(memory_space=pltpu.VMEM)],
         out_specs=pl.BlockSpec(memory_space=pltpu.VMEM),
-        out_shape=jax.ShapeDtypeStruct((8, 128), F32),
+        out_shape=jax.ShapeDtypeStruct((1, PICKS), F32),
         scratch_shapes=[
             pltpu.VMEM((8, 8, 128), F32),
             pltpu.SemaphoreType.DMA((8,)),
@@ -520,10 +478,11 @@
             recv_sem=near_recv.at[i, w], device_id=target, device_id_type=MESH,
         )
 
-    def bulk_copy(w, target):
+    def bulk_copy(part, w, target):
+        cols = pl.ds(pl.multiple_of(part * 2048, 2048), 2048)
         return pltpu.make_async_remote_copy(
-            src_ref=ahead.at[w], dst_ref=bulk.at[w], send_sem=bulk_send.at[w],
-            recv_sem=bulk_recv.at[w], device_id=target, device_id_type=MESH,
+            src_ref=ahead.at[w, :, cols], dst_ref=bulk.at[w, :, cols], send_sem=bulk_send.at[part, w],
+            recv_sem=bulk_recv.at[part, w], device_id=target, device_id_type=MESH,
         )
 
     def tail_copies(w):
@@ -560,10 +519,13 @@
                 sums[1] + jnp.dot(piece, full[1, cs, :], preferred_element_type=F32),
             )
 
+        def deep_part(part, sums):
+            bulk_copy(part, w, {"section": sec}).wait_recv()
+            return lax.fori_loop(2 * part, 2 * part + 2, deep, sums)
+
         def from_bulk():
-            bulk_copy(w, {"section": sec}).wait_recv()
             zero = jnp.zeros((ROWS, HALF), F32)
-            return lax.fori_loop(0, 8, deep, (zero, zero))
+            return lax.fori_loop(0, 4, deep_part, (zero, zero))
 
         def from_start():
             return (start[0, w], start[1, w])
@@ -628,11 +590,16 @@
                 ahead[w, :, cs] = (v_ref[3, row, :] * now + y0).astype(BF16)
             return carry
 
-        lax.fori_loop(0, 8, assemble, 0)
-
-        @pl.when(sec + 4 < sections)
-        def _():
-            bulk_copy(w, {"section": sec + 4}).start()
+        def assemble_part(part, carry):
+            lax.fori_loop(2 * part, 2 * part + 2, assemble, 0)
+
+            @pl.when(sec + 4 < sections)
+            def _():
+                bulk_copy(part, w, {"section": sec + 4}).start()
+
+            return carry
+
+        lax.fori_loop(0, 4, assemble_part, 0)
 
         local, remote = tail_copies(w)
         for copy in remote + local:
@@ -654,7 +621,8 @@
 
         @pl.when(sec + 4 < sections)
         def _():
-            bulk_copy(w, {"section": sec + 4}).wait_send()
+            for part in range(4):
+                bulk_copy(part, w, {"section": sec + 4}).wait_send()
 
         local, remote = tail_copies(w)
         for copy in local:
@@ -693,8 +661,8 @@
             dma((2, MICRO)),
             dma((3, MICRO)),
             dma((3, MICRO)),
-            dma((MICRO,)),
-            dma((MICRO,)),
+            dma((4, MICRO)),
+            dma((4, MICRO)),
             dma((2, MICRO)),
             dma((2, MICRO)),
             dma((2, MICRO)),
@@ -715,27 +683,26 @@
     count = sum(jnp.where(sec >= least, 1, 0) for least in BEFORE).astype(jnp.int32)
     counts = range(PICKS + 1)
     delta = lax.switch(count, [
-        functools.partial(deltas, n, grid_picks, bins, weight, first) if n else lambda: nothing(first)
+        functools.partial(deltas, 0, n, grid_picks, bins, weight, first) if n else lambda: nothing(first)
         for n in counts
     ])
     quant_out, stream = chain(inputs, quant, folds, first, gains, delta)
     stream = stream.reshape(4, MICRO * 32, D // 4)
-    blank = jnp.zeros((8, 128), F32)
-    before, later = lax.switch(count, [
-        functools.partial(
-            lambda n: (
-                losses(n, stream, delta) if n else blank,
-                fused(n, grid_picks, bins, weight, stream) if n < PICKS else blank,
-            ),
-            n,
-        )
-        for n in counts
-    ])
-    part = jnp.where(jnp.arange(8)[:, None] < count, before, later)
-    total = reduce_all(part)
+
+    def part(n):
+        rest = PICKS - n
+        rows = []
+        if rest:
+            rows.append(losses(rest, stream, deltas(n, rest, grid_picks, bins, weight, stream))[:rest])
+        if n:
+            rows.insert(0, losses(n, stream, delta)[:n])
+        rows.append(jnp.zeros((8 - PICKS, 128), F32))
+        return jnp.concatenate(rows)
+
+    total = lax.switch(count, [functools.partial(part, n) for n in counts])
     entry_count = inputs.shape[0] * inputs.shape[1] * lax.axis_size("dp") * KV
-    grid_loss = jnp.sum(total[:PICKS], axis=1) * (LOSS_UNIT / entry_count)
-    return (quant_out[None], grid_loss[None])
+    grid_loss = reduce_all(LOSS_UNIT / entry_count, total)
+    return (quant_out[None], grid_loss)
 
 
 def solution(mesh):

time: 205 us -> 199 us (0.971)
  Pallas kernels: 201 us -> 195 us
    pallas_call x3, Pallas kernels: 92.4 us -> 87.7 us  [the longest x1 66.9 us: deltas(): pl.pallas_call(functools.partial(deltas_body, low), grid=(count, 8), in_s...]
where the time goes in v4:
time: 199 us; the launch traced here: 198 us
  Pallas kernels  195 us (98%)
    pallas_call x1, Pallas kernels, chain(): pl.pallas_call(chain_body, in_specs=[anywhere, anywhere, anywhere, anywhe...  69.5 us
    pallas_call x1, Pallas kernels, deltas(): pl.pallas_call(functools.partial(deltas_body, low), grid=(count, 8), in_s...  66.9 us
    pallas_call x1, Pallas kernels, first_pick(): pl.pallas_call(first_body, grid=(8,), in_specs=[pl.BlockSpec(memory_space...  30.9 us
    pallas_call x1, Pallas kernels, losses(): pl.pallas_call(losses_body, grid=(count, 2), in_specs=[pl.BlockSpec((4, 1...  14.2 us
    pallas_call x1, Pallas kernels, reduce_all(): pl.pallas_call(functools.partial(reduce_body, unit), in_specs=[pl.BlockSp...  6.51 us
    pallas_call x1, Pallas kernels, gains_of(): pl.pallas_call(gains_body, in_specs=[pl.BlockSpec(memory_space=pltpu.VMEM...  6.43 us

profile of v4, /device:TPU:249, one launch (start us, length us, event | category | flops | bytes accessed | tf_op | source)
XLA Modules:
  0.0 198.0 jit_solution(17508244236755188682)
XLA Ops:
  0.7 6.4 %gains.1.g_ref.v_ref = f32[4,64,128]{2,1,0:T(8,128)} custom-call(f32[64,128]{1,0:T(8,128)} %bitcast.29), custom_call_target="tpu_custom_call" | custom-call | tf_op jit(solution)/shard_map/gains/pallas_call | solution.py:341
  7.1 30.9 %first_pick.1 = (bf16[2,8192,512]{2,1,0:T(8,128)(2,1)}, bf16[2,3,1024,512]{3,2,1,0:T(8,128)(2,1)}, f32[2,4,16,512]{3,2,1,0:T(8,128)S(1)}) custom-call(s32[1,20]{1,0:T(1,128)} %picks_ref.1, s32[64,128]{1,0:T(8,128)} %bitcast.19, f32[4,64,128]{2,1,0:T(8,128)} %gains.1.g_ref.v_ref, bf16[8192,512]{1,0:T(8,128)(2,1)} %bitcast.5, bf16[4,32,8192]{2,1,0:T(8,128)(2,1)} %x_ref.3), custom_call_target="tpu_custom_call" | custom-call | tf_op jit(solution)/shard_map/first_pick/pallas_call | solution.py:177
  38.0 67.0 %conditional.2 = (bf16[4,8192,512]{2,1,0:T(8,128)(2,1)}) conditional(s32[]{:T(128)} %clamp.4, f32[2,4,16,512]{3,2,1,0:T(8,128)S(1)} %get-tuple-element.133.a_ref, (s32[1,20]{1,0:T(1,128)}, s32[64,128]{1,0:T(8,128)}, bf16[8192,512]{1,0:T(8,128)(2,1)}, f32[2,4,16,512]{3,2,1,0:T(8,128)S(1)}) %tuple.68, ...), branch_computations={%region_0.1_spmd, %region_1.2_spmd, %region_2.3_spmd, %region_3.4_... | conditional | bytes 8 | solution.py:685
  38.1 66.9 %deltas.11 = bf16[4,8192,512]{2,1,0:T(8,128)(2,1)} custom-call(s32[1,20]{1,0:T(1,128)} %get-tuple-element.99.picks_ref, s32[64,128]{1,0:T(8,128)} %get-tuple-element.100.bins_ref, bf16[8192,512]{1,0:T(8,128)(2,1)} %get-tuple-element.101.w_ref, f32[2,4,16,512]{3,2,1,0:T(8,128)S(1)} %get-tuple-element.102.after_ref), custom_call_target="tpu_custom_call" | custom-call | tf_op jit(solution)/shard_map/cond/branch_4_fun/deltas/pallas_call | solution.py:223
  105.0 0.0 copy-start
  105.0 0.0 copy-start.2
  105.0 69.5 %chain.1 = (bf16[4,32,512]{2,1,0:T(8,128)(2,1)}, bf16[4,4,32,2048]{3,2,1,0:T(8,128)(2,1)S(1)}) custom-call(bf16[4,32,8192]{2,1,0:T(8,128)(2,1)} %x_ref.3, bf16[2,8192,512]{2,1,0:T(8,128)(2,1)} %get-tuple-element.131.q_ref, bf16[2,3,1024,512]{3,2,1,0:T(8,128)(2,1)} %get-tuple-element.132.m_ref, f32[2,4,16,512]{3,2,1,0:T(8,128)S(1)} %get-tuple-element.133.a_ref, ...), custom_call_target="tpu_custom_call" | custom-call | tf_op jit(solution)/shard_map/chain/pallas_call | solution.py:639
  174.6 0.0 copy-done
  174.6 0.0 copy-done.2
  174.6 0.0 copy-start.1
  174.6 15.1 %conditional.3 = (f32[8,128]{1,0:T(8,128)S(1)}) conditional(s32[]{:T(128)} %clamp.4, (s32[1,20]{1,0:T(1,128)S(1)}, s32[64,128]{1,0:T(8,128)S(1)}, bf16[8192,512]{1,0:T(8,128)(2,1)}, bf16[4,128,2048]{2,1,0:T(8,128)(2,1)S(1)}) %tuple.76, (bf16[4,128,2048]{2,1,0:T(8,128)(2,1)S(1)}, bf16[4,8192,512]{2,1,0:T(8,128)(2,1)}, ...), branch_computations={%region_5.6_spmd, %region_6.7_spmd, %region_7.8_spmd, %region_8.9_... | conditional | flops 2048 | bytes 12936 | solution.py:702
  174.6 0.0 copy-start.4
  174.6 14.2 %losses.15 = f32[8,128]{1,0:T(8,128)} custom-call(bf16[4,128,2048]{2,1,0:T(8,128)(2,1)S(1)} %get-tuple-element.122.s_ref, bf16[4,8192,512]{2,1,0:T(8,128)(2,1)} %get-tuple-element.123.refs_0_.refs_1_.refs_2_.refs_3_, bf16[4,8192,512]{2,1,0:T(8,128)(2,1)} %get-tuple-element.123.refs_0_.refs_1_.refs_2_.refs_3_, ...), custom_call_target="tpu_custom_call" | custom-call | tf_op jit(solution)/shard_map/cond/branch_4_fun/losses/pallas_call | solution.py:279
  188.9 0.0 copy-done.4
  188.9 0.8 broadcast_select_fusion.1
  189.7 6.5 %reduce_all.1 = f32[1,4]{1,0:T(1,128)} custom-call(f32[8,128]{1,0:T(8,128)S(1)} %get-tuple-element.141.x_ref), custom_call_target="tpu_custom_call" | custom-call | tf_op jit(solution)/shard_map/reduce_all/pallas_call | solution.py:392
  196.2 0.0 copy-done.1
  196.2 0.7 copy.19
  196.8 1.2 copy.20
Async XLA Ops:
  105.0 69.6 %copy-start = (s32[1,8192]{1,0:T(1,128)S(1)}, s32[1,8192]{1,0:T(1,128)}, u32[]{:S(2)}) copy-start(s32[1,8192]{1,0:T(1,128)} %param.18) | copy-start | bytes 98308
  105.0 69.6 %copy-start.2 = (s32[1,20]{1,0:T(1,128)S(1)}, s32[1,20]{1,0:T(1,128)}, u32[]{:S(2)}) copy-start(s32[1,20]{1,0:T(1,128)} %picks_ref.1) | copy-start | bytes 244
  174.6 21.6 %copy-start.1 = (bf16[4,32,512]{2,1,0:T(8,128)(2,1)S(1)}, bf16[4,32,512]{2,1,0:T(8,128)(2,1)}, u32[]{:S(2)}) copy-start(bf16[4,32,512]{2,1,0:T(8,128)(2,1)} %get-tuple-element.134) | copy-start | bytes 393220
  174.6 14.3 %copy-start.4 = (pred[8]{0:T(512)(128)(4,1)S(1)}, pred[8]{0:T(512)(128)(4,1)}, u32[]{:S(2)}) copy-start(pred[8]{0:T(512)(128)(4,1)} %constant.8.clone) | copy-start | bytes 28 | tf_op jit(solution)/shard_map/cond

commit v5 on v4

--- a/solution.py
+++ b/solution.py
@@ -17,7 +17,7 @@
 PICKS = 4
 MICRO = 4
 ROWS = 16
-BEFORE = (9, 14, 20, 25)
+BEFORE = (10, 15, 20, 25)
 
 EPS = 1e-06
 LOSS_UNIT = 1000.0
@@ -455,11 +455,9 @@
 
     a_copy.wait()
 
-    @pl.when(sec < 4)
-    def _():
-        x_copy.wait()
-
-    m_copy.wait()
+    @pl.when(sec >= 1)
+    def _():
+        m_copy.wait()
 
     @pl.when(sec >= 4)
     def _():
@@ -575,6 +573,10 @@
             def _():
                 near_copy(i, w, {"section": sec + i + 1}).start()
 
+        @pl.when((sec < 4) & (w == 0))
+        def _():
+            x_copy.wait()
+
         def assemble(c, carry):
             heads = pl.ds(pl.multiple_of(c * HEAD, HEAD), HEAD)
             y1 = near[0, w, :, heads].astype(F32) * root
@@ -632,6 +634,10 @@
         return carry
 
     lax.fori_loop(0, MICRO, finish, 0)
+
+    @pl.when(sec < 1)
+    def _():
+        m_copy.wait()
 
 def chain(inputs, quant, folds, first, vectors, after):
     anywhere = pl.BlockSpec(memory_space=pl.ANY)

time: 199 us -> 197 us (0.990)
  Pallas kernels: 195 us -> 192 us
    pallas_call x1, Pallas kernels: 69.5 us -> 67.2 us  [chain(): pl.pallas_call(chain_body, in_specs=[anywhere, anywhere, anywhere, anywhe...]
where the time goes in v5:
time: 197 us; the launch traced here: 196 us
  Pallas kernels  192 us (97%)
    pallas_call x1, Pallas kernels, chain(): pl.pallas_call(chain_body, in_specs=[anywhere, anywhere, anywhere, anywhe...  67.2 us
    pallas_call x1, Pallas kernels, deltas(): pl.pallas_call(functools.partial(deltas_body, low), grid=(count, 8), in_s...  66.9 us
    pallas_call x1, Pallas kernels, first_pick(): pl.pallas_call(first_body, grid=(8,), in_specs=[pl.BlockSpec(memory_space...  30.9 us
    pallas_call x1, Pallas kernels, losses(): pl.pallas_call(losses_body, grid=(count, 2), in_specs=[pl.BlockSpec((4, 1...  14.2 us
    pallas_call x1, Pallas kernels, reduce_all(): pl.pallas_call(functools.partial(reduce_body, unit), in_specs=[pl.BlockSp...  6.52 us
    pallas_call x1, Pallas kernels, gains_of(): pl.pallas_call(gains_body, in_specs=[pl.BlockSpec(memory_space=pltpu.VMEM...  6.43 us

profile of v5, /device:TPU:249, one launch (start us, length us, event | category | flops | bytes accessed | tf_op | source)
XLA Modules:
  0.0 195.7 jit_solution(11470650477333217507)
XLA Ops:
  0.7 6.4 %gains.1.g_ref.v_ref = f32[4,64,128]{2,1,0:T(8,128)} custom-call(f32[64,128]{1,0:T(8,128)} %bitcast.29), custom_call_target="tpu_custom_call" | custom-call | tf_op jit(solution)/shard_map/gains/pallas_call | solution.py:341
  7.1 30.9 %first_pick.1 = (bf16[2,8192,512]{2,1,0:T(8,128)(2,1)}, bf16[2,3,1024,512]{3,2,1,0:T(8,128)(2,1)}, f32[2,4,16,512]{3,2,1,0:T(8,128)S(1)}) custom-call(s32[1,20]{1,0:T(1,128)} %picks_ref.1, s32[64,128]{1,0:T(8,128)} %bitcast.19, f32[4,64,128]{2,1,0:T(8,128)} %gains.1.g_ref.v_ref, bf16[8192,512]{1,0:T(8,128)(2,1)} %bitcast.5, bf16[4,32,8192]{2,1,0:T(8,128)(2,1)} %x_ref.3), custom_call_target="tpu_custom_call" | custom-call | tf_op jit(solution)/shard_map/first_pick/pallas_call | solution.py:177
  38.0 67.0 %conditional.2 = (bf16[4,8192,512]{2,1,0:T(8,128)(2,1)}) conditional(s32[]{:T(128)} %clamp.4, f32[2,4,16,512]{3,2,1,0:T(8,128)S(1)} %get-tuple-element.133.a_ref, (s32[1,20]{1,0:T(1,128)}, s32[64,128]{1,0:T(8,128)}, bf16[8192,512]{1,0:T(8,128)(2,1)}, f32[2,4,16,512]{3,2,1,0:T(8,128)S(1)}) %tuple.68, ...), branch_computations={%region_0.1_spmd, %region_1.2_spmd, %region_2.3_spmd, %region_3.4_... | conditional | bytes 8 | solution.py:691
  38.1 66.9 %deltas.11 = bf16[4,8192,512]{2,1,0:T(8,128)(2,1)} custom-call(s32[1,20]{1,0:T(1,128)} %get-tuple-element.99.picks_ref, s32[64,128]{1,0:T(8,128)} %get-tuple-element.100.bins_ref, bf16[8192,512]{1,0:T(8,128)(2,1)} %get-tuple-element.101.w_ref, f32[2,4,16,512]{3,2,1,0:T(8,128)S(1)} %get-tuple-element.102.after_ref), custom_call_target="tpu_custom_call" | custom-call | tf_op jit(solution)/shard_map/cond/branch_4_fun/deltas/pallas_call | solution.py:223
  105.0 0.0 copy-start
  105.0 0.0 copy-start.2
  105.0 67.2 %chain.1 = (bf16[4,32,512]{2,1,0:T(8,128)(2,1)}, bf16[4,4,32,2048]{3,2,1,0:T(8,128)(2,1)S(1)}) custom-call(bf16[4,32,8192]{2,1,0:T(8,128)(2,1)} %x_ref.3, bf16[2,8192,512]{2,1,0:T(8,128)(2,1)} %get-tuple-element.131.q_ref, bf16[2,3,1024,512]{3,2,1,0:T(8,128)(2,1)} %get-tuple-element.132.m_ref, f32[2,4,16,512]{3,2,1,0:T(8,128)S(1)} %get-tuple-element.133.a_ref, ...), custom_call_target="tpu_custom_call" | custom-call | tf_op jit(solution)/shard_map/chain/pallas_call | solution.py:645
  172.2 0.0 copy-done
  172.2 0.0 copy-done.2
  172.2 0.0 copy-start.1
  172.2 15.1 %conditional.3 = (f32[8,128]{1,0:T(8,128)S(1)}) conditional(s32[]{:T(128)} %clamp.4, (s32[1,20]{1,0:T(1,128)S(1)}, s32[64,128]{1,0:T(8,128)S(1)}, bf16[8192,512]{1,0:T(8,128)(2,1)}, bf16[4,128,2048]{2,1,0:T(8,128)(2,1)S(1)}) %tuple.76, (bf16[4,128,2048]{2,1,0:T(8,128)(2,1)S(1)}, bf16[4,8192,512]{2,1,0:T(8,128)(2,1)}, ...), branch_computations={%region_5.6_spmd, %region_6.7_spmd, %region_7.8_spmd, %region_8.9_... | conditional | flops 2048 | bytes 12936 | solution.py:708
  172.3 0.0 copy-start.4
  172.3 14.2 %losses.15 = f32[8,128]{1,0:T(8,128)} custom-call(bf16[4,128,2048]{2,1,0:T(8,128)(2,1)S(1)} %get-tuple-element.122.s_ref, bf16[4,8192,512]{2,1,0:T(8,128)(2,1)} %get-tuple-element.123.refs_0_.refs_1_.refs_2_.refs_3_, bf16[4,8192,512]{2,1,0:T(8,128)(2,1)} %get-tuple-element.123.refs_0_.refs_1_.refs_2_.refs_3_, ...), custom_call_target="tpu_custom_call" | custom-call | tf_op jit(solution)/shard_map/cond/branch_4_fun/losses/pallas_call | solution.py:279
  186.5 0.0 copy-done.4
  186.5 0.8 broadcast_select_fusion.1
  187.3 6.5 %reduce_all.1 = f32[1,4]{1,0:T(1,128)} custom-call(f32[8,128]{1,0:T(8,128)S(1)} %get-tuple-element.141.x_ref), custom_call_target="tpu_custom_call" | custom-call | tf_op jit(solution)/shard_map/reduce_all/pallas_call | solution.py:392
  193.8 0.0 copy-done.1
  193.8 0.7 copy.19
  194.5 1.2 copy.20
Async XLA Ops:
  105.0 67.2 %copy-start = (s32[1,8192]{1,0:T(1,128)S(1)}, s32[1,8192]{1,0:T(1,128)}, u32[]{:S(2)}) copy-start(s32[1,8192]{1,0:T(1,128)} %param.18) | copy-start | bytes 98308
  105.0 67.2 %copy-start.2 = (s32[1,20]{1,0:T(1,128)S(1)}, s32[1,20]{1,0:T(1,128)}, u32[]{:S(2)}) copy-start(s32[1,20]{1,0:T(1,128)} %picks_ref.1) | copy-start | bytes 244
  172.2 21.6 %copy-start.1 = (bf16[4,32,512]{2,1,0:T(8,128)(2,1)S(1)}, bf16[4,32,512]{2,1,0:T(8,128)(2,1)}, u32[]{:S(2)}) copy-start(bf16[4,32,512]{2,1,0:T(8,128)(2,1)} %get-tuple-element.134) | copy-start | bytes 393220
  172.3 14.3 %copy-start.4 = (pred[8]{0:T(512)(128)(4,1)S(1)}, pred[8]{0:T(512)(128)(4,1)}, u32[]{:S(2)}) copy-start(pred[8]{0:T(512)(128)(4,1)} %constant.8.clone) | copy-start | bytes 28 | tf_op jit(solution)/shard_map/cond
